TPU v7x, 512 devices: a 4x2x32 block of a 4x8x32 slice. The times are simulated.
512 devices in a mesh: sweep: 2 (over y), row: 8 (over x, core), col: 32 (over z).
Axes of the slice: x: 4, y: 2, z: 32, core: 2. Of those that a mesh axis runs over, the one named last changes fastest.
The devices are a block of a 4x8x32 slice.
Arguments:
- tokens: bfloat16 [1280, 4096], P(('sweep', 'col'), 'row'), parts along dimension 0, may hold values from -6 to 6
- w_gate: bfloat16 [4096, 14336], P('row', 'col'), may hold values from -0.09375 to 0.09375
- w_up: bfloat16 [4096, 14336], P('row', 'col'), may hold values from -0.09375 to 0.09375
- w_down: bfloat16 [14336, 4096], P('col', 'row'), may hold values from -0.046875 to 0.046875
- cotangent: bfloat16 [1280, 4096], P(('sweep', 'col'), 'row'), parts along dimension 0, may hold values from -6 to 6
- step_rate: float32 [2], P('sweep'), parts along dimension 0, may hold values from 0.05 to 0.3
Outputs:
- out_rows: bfloat16 [1280, 4096], P(('sweep', 'col'), 'row'), parts along dimension 0
- grad_in: bfloat16 [1280, 4096], P(('sweep', 'col'), 'row'), parts along dimension 0
- step_gate: bfloat16 [8192, 14336], P(('sweep', 'row'), 'col'), parts along dimension 0
- step_up: bfloat16 [8192, 14336], P(('sweep', 'row'), 'col'), parts along dimension 0
- step_down: bfloat16 [28672, 4096], P(('sweep', 'col'), 'row'), parts along dimension 0
There are 2 independent parts, one for each index of `sweep`. A program takes and returns all parts, laid end to end along the dimension named above; an argument that names none is the same for every part. Nothing has to cross between parts.
All inputs are finite; a program needn't handle non-finite values.
Results may differ from a plain program's by a relative error of at most 0.0049.
Values may be sent and summed in bfloat16 or wider, within the bound.
No kernel may reach another device: no remote copies, remote signals or barrier semaphores. Data moves between devices by JAX's collectives and lax.ppermute only.
A program may use at most 64 MiB of HBM per device.

v0:
```python
import jax
import jax.numpy as jnp
from jax import lax
from jax.sharding import PartitionSpec as P


def cut_along(value, dim, count):
    before, after = (value.shape[:dim], value.shape[dim + 1 :])
    return jnp.moveaxis(value.reshape(*before, count, -1, *after), dim, 0)


def summed_on_arrival(value, axis, dim):
    count = lax.axis_size(axis)
    parts = lax.all_to_all(cut_along(value, dim, count), axis, 0, 0, tiled=True)
    return jnp.sum(parts, axis=0)


def swiglu_back(back_hidden, gate_val, up_val):
    gate_sig = jax.nn.sigmoid(gate_val)
    activation = gate_val * gate_sig
    back_gate = (back_hidden * up_val * gate_sig * (1.0 + gate_val * (1.0 - gate_sig))).astype(
        jnp.bfloat16
    )
    back_up = (back_hidden * activation).astype(jnp.bfloat16)
    return (back_gate, back_up)


def forward_hidden(gate_val, up_val):
    gate_sig = jax.nn.sigmoid(gate_val)
    return (gate_val * gate_sig * up_val).astype(jnp.bfloat16)


def contract_last(left, right):
    return lax.dot_general(
        left, right, (((1,), (1,)), ((), ())), preferred_element_type=jnp.float32
    )


def contract_first(left, right):
    return lax.dot_general(
        left, right, (((0,), (0,)), ((), ())), preferred_element_type=jnp.float32
    )


def local(tokens, w_gate, w_up, w_down, cotangent, step_rate):
    tokens_all = lax.all_gather(tokens, "col", axis=0, tiled=True)
    hidden_width = w_gate.shape[1]
    w_both = jnp.concatenate([w_gate, w_up], axis=1)
    picked = tokens_all
    summed = summed_on_arrival(
        jnp.dot(picked, w_both, preferred_element_type=jnp.float32), "row", 0
    )
    gate_val = summed[:, :hidden_width]
    up_val = summed[:, hidden_width:]
    hidden = forward_hidden(gate_val, up_val)
    hidden_all = lax.all_gather(hidden, "row", axis=0, tiled=True)
    picked = hidden_all
    branch_out = lax.psum_scatter(
        jnp.dot(picked, w_down, preferred_element_type=jnp.float32),
        "col",
        scatter_dimension=0,
        tiled=True,
    )
    out_rows = (tokens.astype(jnp.float32) + branch_out).astype(jnp.bfloat16)
    cotangent_all = lax.all_gather(cotangent, "col", axis=0, tiled=True)
    picked = cotangent_all
    back_hidden = lax.psum_scatter(
        contract_last(picked, w_down), "row", scatter_dimension=0, tiled=True
    )
    back_gate, back_up = swiglu_back(back_hidden, gate_val, up_val)
    gate_grad_all, up_grad_all = (
        lax.all_gather(back_gate, "row", axis=0, tiled=True),
        lax.all_gather(back_up, "row", axis=0, tiled=True),
    )
    grads_all = jnp.concatenate([gate_grad_all, up_grad_all], axis=1)
    picked = grads_all
    input_sums = lax.psum_scatter(
        contract_last(picked, w_both), "col", scatter_dimension=0, tiled=True
    )
    grad_in = (cotangent.astype(jnp.float32) + input_sums).astype(jnp.bfloat16)
    factor = -step_rate[0]
    weight_grads = contract_first(tokens_all, grads_all)
    step_gate = (factor * weight_grads[:, :hidden_width]).astype(jnp.bfloat16)
    step_up = (factor * weight_grads[:, hidden_width:]).astype(jnp.bfloat16)
    step_down = (factor * contract_first(hidden_all, cotangent_all)).astype(jnp.bfloat16)
    return (out_rows, grad_in, step_gate, step_up, step_down)


def solution(mesh):
    in_specs = (
        P(("sweep", "col"), "row"),
        P("row", "col"),
        P("row", "col"),
        P("col", "row"),
        P(("sweep", "col"), "row"),
        P("sweep"),
    )
    out_specs = (
        P(("sweep", "col"), "row"),
        P(("sweep", "col"), "row"),
        P(("sweep", "row"), "col"),
        P(("sweep", "row"), "col"),
        P(("sweep", "col"), "row"),
    )
    return jax.shard_map(local, mesh=mesh, in_specs=in_specs, out_specs=out_specs, check_vma=False)
```

profile of v0, /device:TPU:40, one launch (start us, length us, event | category | flops | bytes accessed | tf_op | source)
XLA Modules:
  0.0 388.1 jit_solution(322608121071958712)
XLA Ops:
  7.2 0.0 copy-start
  7.2 0.1 reduce-scatter.6.cloned.1.call-start
  7.3 99.7 %all-gather.1 = bf16[32,20,512]{2,1,0:T(8,128)(2,1)S(1)} all-gather(bf16[1,20,512]{2,1,0:T(8,128)(2,1)} %bitcast.24), channel_id=1, replica_groups=mesh['sweep'=2,'row'=8,'col'=32] {'col'}, dimensions={0}, use_global_device_ids=true | all-gather | bytes 675840 | tf_op jit(solution)/shard_map/all_gather | solution.py:65
  106.9 0.1 reshape.18
  107.1 0.0 copy-done
  107.1 0.0 copy-start.3
  107.1 0.0 copy-start.7
  107.1 1.6 fusion.14
  108.7 0.0 copy-done.3
  108.7 0.1 reduce-scatter.6.cloned.1.call-update
  108.8 0.0 copy-done.7
  108.8 0.0 copy-start.8
  108.8 0.6 copy-done.10
  109.5 55.4 %all-gather = bf16[32,20,512]{2,1,0:T(8,128)(2,1)S(1)} all-gather(bf16[1,20,512]{2,1,0:T(8,128)(2,1)S(1)} %bitcast.25), channel_id=1, replica_groups=mesh['sweep'=2,'row'=8,'col'=32] {'col'}, dimensions={0}, use_global_device_ids=true | all-gather | bytes 675840 | tf_op jit(solution)/shard_map/all_gather | solution.py:46
  164.9 0.1 reshape.16
  165.0 0.0 copy-done.8
  165.1 0.0 copy-start.1
  165.1 2.3 fusion.12
  167.4 0.0 copy-done.1
  167.4 4.6 %all-to-all-start = ((f32[8,80,896]{2,1,0:T(8,128)}), f32[8,80,896]{2,1,0:T(8,128)S(1)}, u32[]{:S(2)}, u32[]{:S(2)}) async-start(f32[8,80,896]{2,1,0:T(8,128)} %bitcast.2), calls=%async_computation | async-start | bytes 4587520 | tf_op jit(solution)/shard_map/all_to_all | solution.py:14
  172.7 1.3 dynamic-slice.6
  174.6 26.7 %all-to-all-done = f32[8,80,896]{2,1,0:T(8,128)S(1)} async-done(((f32[8,80,896]{2,1,0:T(8,128)}), f32[8,80,896]{2,1,0:T(8,128)S(1)}, u32[]{:S(2)}, u32[]{:S(2)}) %all-to-all-start) | async-done | bytes 2293792 | tf_op jit(solution)/shard_map/all_to_all | solution.py:14
  201.3 0.8 reduce_sum.9
  202.1 1.2 multiply_convert_fusion.1
  203.3 13.3 %all_gather.18 = bf16[640,448]{1,0:T(8,128)(2,1)S(1)} all-gather(bf16[80,448]{1,0:T(8,128)(2,1)S(1)} %get-tuple-element.11), channel_id=1, replica_groups=mesh['sweep'=2,'row'=8,'col'=32] {'row'}, dimensions={0}, use_global_device_ids=true | all-gather | bytes 645120 | tf_op jit(solution)/shard_map/all_gather | solution.py:72
  216.6 13.3 %all_gather.19 = bf16[640,448]{1,0:T(8,128)(2,1)S(1)} all-gather(bf16[80,448]{1,0:T(8,128)(2,1)S(1)} %get-tuple-element.12), channel_id=1, replica_groups=mesh['sweep'=2,'row'=8,'col'=32] {'row'}, dimensions={0}, use_global_device_ids=true | all-gather | bytes 645120 | tf_op jit(solution)/shard_map/all_gather | solution.py:73
  229.9 13.4 %all_gather.16 = bf16[640,448]{1,0:T(8,128)(2,1)S(1)} all-gather(bf16[80,448]{1,0:T(8,128)(2,1)S(1)} %get-tuple-element.13), channel_id=1, replica_groups=mesh['sweep'=2,'row'=8,'col'=32] {'row'}, dimensions={0}, use_global_device_ids=true | all-gather | bytes 645120 | tf_op jit(solution)/shard_map/all_gather | solution.py:56
  243.4 0.5 fusion.13
  243.8 0.0 copy-done.5
  243.9 0.0 copy-done.6
  243.9 0.0 copy-done.2
  243.9 1.9 fusion.5
  245.8 70.9 %fusion.11 = (f32[24,512]{1,0:T(8,128)S(1)}, f32[24,512]{1,0:T(8,128)S(1)}) fusion(f32[640,512]{1,0:T(8,128)S(1)} %fusion.13, f32[640,512]{1,0:T(8,128)} %fusion.5), kind=kCustom, calls=%all-reduce-scatter.2 | all-reduce-scatter fusion | flops 786433 | bytes 2721792
  316.7 5.5 %collective-permute-start.10 = (f32[24,512]{1,0:T(8,128)S(1)}, f32[24,512]{1,0:T(8,128)S(1)}, u32[]{:S(2)}, u32[]{:S(2)}) collective-permute-start(f32[24,512]{1,0:T(8,128)S(1)} %get-tuple-element.8), channel_id=1, source_target_pairs={{0,5},{1,6},{2,7},{3,8},{4,9},{5,10},{6,11},{7,12},{8,13},{9,14},{... | collective-permute-start | bytes 147464
  322.2 4.2 %collective-permute-start.6 = (f32[24,512]{1,0:T(8,128)S(1)}, f32[24,512]{1,0:T(8,128)S(1)}, u32[]{:S(2)}, u32[]{:S(2)}) collective-permute-start(f32[24,512]{1,0:T(8,128)S(1)} %get-tuple-element.8), channel_id=1, source_target_pairs={{0,1},{1,2},{2,3},{3,4},{4,5},{5,6},{6,7},{7,8},{8,9},{9,10},{10,1... | collective-permute-start | bytes 147464
  326.4 2.2 collective-permute-start.7
  328.6 3.1 collective-permute-start.8
  331.7 2.4 convolution_bitcast_fusion
  334.1 3.5 collective-permute-start.11
  337.6 1.2 fusion.3
  338.8 0.2 collective-permute-done.11
  338.9 5.2 %collective-permute-start.9 = (f32[24,512]{1,0:T(8,128)S(1)}, f32[24,512]{1,0:T(8,128)S(1)}, u32[]{:S(2)}, u32[]{:S(2)}) collective-permute-start(f32[24,512]{1,0:T(8,128)S(1)} %get-tuple-element.8), channel_id=1, source_target_pairs={{0,4},{1,5},{2,6},{3,7},{4,8},{5,9},{6,10},{7,11},{8,12},{9,13},{1... | collective-permute-start | bytes 147464
  344.1 0.0 collective-permute-done.10
  344.1 9.9 %collective-permute-start.5 = (f32[4,512]{1,0:T(4,128)S(1)}, f32[4,512]{1,0:T(4,128)S(1)}, u32[]{:S(2)}, u32[]{:S(2)}) collective-permute-start(f32[4,512]{1,0:T(4,128)S(1)} %slice.20), channel_id=1, source_target_pairs={{0,6},{1,7},{2,8},{3,9},{4,10},{5,11},{6,12},{7,13},{8,14},{9,15},... | collective-permute-start | bytes 24584
  354.1 1.3 fusion.2
  355.4 0.0 collective-permute-done.6
  355.4 2.8 collective-permute-start
  358.2 0.0 collective-permute-done.7
  358.2 6.5 %collective-permute-start.1 = (f32[24,512]{1,0:T(8,128)S(1)}, f32[24,512]{1,0:T(8,128)S(1)}, u32[]{:S(2)}, u32[]{:S(2)}) collective-permute-start(f32[24,512]{1,0:T(8,128)S(1)} %get-tuple-element.7), channel_id=1, source_target_pairs={{0,2},{1,3},{2,4},{3,5},{4,6},{5,7},{6,8},{7,9},{8,10},{9,11},{10,... | collective-permute-start | bytes 147464
  364.8 0.0 collective-permute-done.8
  364.8 5.2 %collective-permute-start.2 = (f32[24,512]{1,0:T(8,128)S(1)}, f32[24,512]{1,0:T(8,128)S(1)}, u32[]{:S(2)}, u32[]{:S(2)}) collective-permute-start(f32[24,512]{1,0:T(8,128)S(1)} %get-tuple-element.7), channel_id=1, source_target_pairs={{0,3},{1,4},{2,5},{3,6},{4,7},{5,8},{6,9},{7,10},{8,11},{9,12},{10... | collective-permute-start | bytes 147464
  370.0 0.0 collective-permute-done.9
  370.0 5.0 %collective-permute-start.3 = (f32[24,512]{1,0:T(8,128)S(1)}, f32[24,512]{1,0:T(8,128)S(1)}, u32[]{:S(2)}, u32[]{:S(2)}) collective-permute-start(f32[24,512]{1,0:T(8,128)S(1)} %get-tuple-element.7), channel_id=1, source_target_pairs={{0,4},{1,5},{2,6},{3,7},{4,8},{5,9},{6,10},{7,11},{8,12},{9,13},{1... | collective-permute-start | bytes 147464
  375.0 0.9 concatenate.9
  375.9 0.0 collective-permute-done.5
  375.9 2.1 collective-permute-start.4
  378.0 0.6 fusion.7
  378.6 0.0 collective-permute-done
  378.7 0.0 collective-permute-done.1
  378.7 0.0 collective-permute-done.2
  378.7 0.0 collective-permute-done.3
  378.7 1.1 collective-permute-done.4
  379.7 0.8 concatenate.8
  380.6 0.6 fusion.8
  (13 shorter events, 0.1 us)
Async XLA Ops:
  7.2 99.9 %copy-start = (bf16[448,512]{1,0:T(8,128)(2,1)S(1)}, bf16[448,512]{1,0:T(8,128)(2,1)}, u32[]{:S(2)}) copy-start(bf16[448,512]{1,0:T(8,128)(2,1)} %param.9) | copy-start | bytes 1376260
  7.2 194.9 %reduce-scatter.6.cloned.1.call-start = ((), (), s32[]{:S(2)}) async-start(), calls=%async_computation.2 | async-start | bytes 1474560 | tf_op jit(solution)/shard_map/reduce_scatter | solution.py:67
  107.1 1.6 copy-start.3
  107.1 1.7 copy-start.7
  108.7 0.7 copy-start.10
  108.8 56.2 %copy-start.8 = (bf16[512,448]{0,1:T(8,128)(2,1)S(1)}, bf16[512,448]{0,1:T(8,128)(2,1)}, u32[]{:S(2)}) copy-start(bf16[512,448]{0,1:T(8,128)(2,1)} %param.8) | copy-start | bytes 1376260
  165.1 2.3 copy-start.1
  167.4 33.9 %all-to-all-start = ((f32[8,80,896]{2,1,0:T(8,128)}), f32[8,80,896]{2,1,0:T(8,128)S(1)}, u32[]{:S(2)}, u32[]{:S(2)}) async-start(f32[8,80,896]{2,1,0:T(8,128)} %bitcast.2), calls=%async_computation | async-start | bytes 4587520 | tf_op jit(solution)/shard_map/all_to_all | solution.py:14
  216.6 27.2 %copy-start.5 = (bf16[640,448]{1,0:T(8,128)(2,1)}, bf16[640,448]{1,0:T(8,128)(2,1)S(1)}, u32[]{:S(2)}) copy-start(bf16[640,448]{1,0:T(8,128)(2,1)S(1)} %all_gather.18) | copy-start | bytes 1720324
  229.9 13.9 %copy-start.6 = (bf16[640,448]{1,0:T(8,128)(2,1)}, bf16[640,448]{1,0:T(8,128)(2,1)S(1)}, u32[]{:S(2)}) copy-start(bf16[640,448]{1,0:T(8,128)(2,1)S(1)} %all_gather.19) | copy-start | bytes 1720324
  229.9 13.9 %copy-start.2 = (bf16[512,896]{0,1:T(8,128)(2,1)S(1)}, bf16[512,896]{0,1:T(8,128)(2,1)}, u32[]{:S(2)}) copy-start(bf16[512,896]{0,1:T(8,128)(2,1)} %copy-done.1) | copy-start | bytes 2752516
  316.7 27.4 %collective-permute-start.10 = (f32[24,512]{1,0:T(8,128)S(1)}, f32[24,512]{1,0:T(8,128)S(1)}, u32[]{:S(2)}, u32[]{:S(2)}) collective-permute-start(f32[24,512]{1,0:T(8,128)S(1)} %get-tuple-element.8), channel_id=1, source_target_pairs={{0,5},{1,6},{2,7},{3,8},{4,9},{5,10},{6,11},{7,12},{8,13},{9,14},{... | collective-permute-start | bytes 147464
  322.2 33.2 %collective-permute-start.6 = (f32[24,512]{1,0:T(8,128)S(1)}, f32[24,512]{1,0:T(8,128)S(1)}, u32[]{:S(2)}, u32[]{:S(2)}) collective-permute-start(f32[24,512]{1,0:T(8,128)S(1)} %get-tuple-element.8), channel_id=1, source_target_pairs={{0,1},{1,2},{2,3},{3,4},{4,5},{5,6},{6,7},{7,8},{8,9},{9,10},{10,1... | collective-permute-start | bytes 147464
  326.4 31.8 %collective-permute-start.7 = (f32[24,512]{1,0:T(8,128)S(1)}, f32[24,512]{1,0:T(8,128)S(1)}, u32[]{:S(2)}, u32[]{:S(2)}) collective-permute-start(f32[24,512]{1,0:T(8,128)S(1)} %get-tuple-element.8), channel_id=1, source_target_pairs={{0,2},{1,3},{2,4},{3,5},{4,6},{5,7},{6,8},{7,9},{8,10},{9,11},{10,... | collective-permute-start | bytes 147464
  328.6 36.1 %collective-permute-start.8 = (f32[24,512]{1,0:T(8,128)S(1)}, f32[24,512]{1,0:T(8,128)S(1)}, u32[]{:S(2)}, u32[]{:S(2)}) collective-permute-start(f32[24,512]{1,0:T(8,128)S(1)} %get-tuple-element.8), channel_id=1, source_target_pairs={{0,3},{1,4},{2,5},{3,6},{4,7},{5,8},{6,9},{7,10},{8,11},{9,12},{10... | collective-permute-start | bytes 147464
  334.1 20.0 %copy-start.4 = (bf16[640,512]{1,0:T(8,128)(2,1)S(1)}, bf16[640,512]{1,0:T(8,128)(2,1)}, u32[]{:S(2)}) copy-start(bf16[640,512]{1,0:T(8,128)(2,1)} %copy-done.3) | copy-start | bytes 1966084
  334.1 4.8 %collective-permute-start.11 = (f32[4,512]{1,0:T(4,128)S(1)}, f32[4,512]{1,0:T(4,128)S(1)}, u32[]{:S(2)}, u32[]{:S(2)}) collective-permute-start(f32[4,512]{1,0:T(4,128)S(1)} %slice.21), channel_id=1, source_target_pairs={{0,6},{1,7},{2,8},{3,9},{4,10},{5,11},{6,12},{7,13},{8,14},{9,15},... | collective-permute-start | bytes 24584
  338.8 39.3 %copy-start.9 = (bf16[20,512]{1,0:T(8,128)(2,1)S(1)}, bf16[20,512]{1,0:T(8,128)(2,1)}, u32[]{:S(2)}) copy-start(bf16[20,512]{1,0:T(8,128)(2,1)} %param.10) | copy-start | bytes 61444
  338.9 31.0 %collective-permute-start.9 = (f32[24,512]{1,0:T(8,128)S(1)}, f32[24,512]{1,0:T(8,128)S(1)}, u32[]{:S(2)}, u32[]{:S(2)}) collective-permute-start(f32[24,512]{1,0:T(8,128)S(1)} %get-tuple-element.8), channel_id=1, source_target_pairs={{0,4},{1,5},{2,6},{3,7},{4,8},{5,9},{6,10},{7,11},{8,12},{9,13},{1... | collective-permute-start | bytes 147464
  344.1 31.8 %collective-permute-start.5 = (f32[4,512]{1,0:T(4,128)S(1)}, f32[4,512]{1,0:T(4,128)S(1)}, u32[]{:S(2)}, u32[]{:S(2)}) collective-permute-start(f32[4,512]{1,0:T(4,128)S(1)} %slice.20), channel_id=1, source_target_pairs={{0,6},{1,7},{2,8},{3,9},{4,10},{5,11},{6,12},{7,13},{8,14},{9,15},... | collective-permute-start | bytes 24584
  355.4 23.2 %collective-permute-start = (f32[24,512]{1,0:T(8,128)S(1)}, f32[24,512]{1,0:T(8,128)S(1)}, u32[]{:S(2)}, u32[]{:S(2)}) collective-permute-start(f32[24,512]{1,0:T(8,128)S(1)} %get-tuple-element.7), channel_id=1, source_target_pairs={{0,1},{1,2},{2,3},{3,4},{4,5},{5,6},{6,7},{7,8},{8,9},{9,10},{10,1... | collective-permute-start | bytes 147464
  358.2 20.5 %collective-permute-start.1 = (f32[24,512]{1,0:T(8,128)S(1)}, f32[24,512]{1,0:T(8,128)S(1)}, u32[]{:S(2)}, u32[]{:S(2)}) collective-permute-start(f32[24,512]{1,0:T(8,128)S(1)} %get-tuple-element.7), channel_id=1, source_target_pairs={{0,2},{1,3},{2,4},{3,5},{4,6},{5,7},{6,8},{7,9},{8,10},{9,11},{10,... | collective-permute-start | bytes 147464
  364.8 13.9 %collective-permute-start.2 = (f32[24,512]{1,0:T(8,128)S(1)}, f32[24,512]{1,0:T(8,128)S(1)}, u32[]{:S(2)}, u32[]{:S(2)}) collective-permute-start(f32[24,512]{1,0:T(8,128)S(1)} %get-tuple-element.7), channel_id=1, source_target_pairs={{0,3},{1,4},{2,5},{3,6},{4,7},{5,8},{6,9},{7,10},{8,11},{9,12},{10... | collective-permute-start | bytes 147464
  370.0 8.7 %collective-permute-start.3 = (f32[24,512]{1,0:T(8,128)S(1)}, f32[24,512]{1,0:T(8,128)S(1)}, u32[]{:S(2)}, u32[]{:S(2)}) collective-permute-start(f32[24,512]{1,0:T(8,128)S(1)} %get-tuple-element.7), channel_id=1, source_target_pairs={{0,4},{1,5},{2,6},{3,7},{4,8},{5,9},{6,10},{7,11},{8,12},{9,13},{1... | collective-permute-start | bytes 147464
  375.9 3.8 collective-permute-start.4
Sparse Core Ops, SparseCore 0:
  108.9 32.3 reduce-scatter.5
where the time goes:
time: 389 us; the launch traced here: 388 us
  blocking collectives  266 us (68%)
  starting transfers between devices  59.9 us (15%)
  waiting for transfers between devices  28 us (7%)
  between operations  15.7 us (4%)
  matrix products  10 us (3%)
  other arithmetic  4.44 us (1%)
  local copies, waits for them, and re-layouts  3.94 us (1%)
    all_gather x1, blocking collectives, local(): cotangent_all = lax.all_gather(cotangent, 'col', axis=0, tiled=True)  99.7 us
    unnamed x1, blocking collectives  70.9 us
    all_gather x1, blocking collectives, local(): tokens_all = lax.all_gather(tokens, 'col', axis=0, tiled=True)  55.4 us
    unnamed x12, starting transfers between devices  55.2 us
    all_to_all x1, waiting for transfers between devices, summed_on_arrival(): parts = lax.all_to_all(cut_along(value, dim, count), axis, 0, 0, tiled=True)  26.7 us
    all_gather x1, blocking collectives, local(): hidden_all = lax.all_gather(hidden, 'row', axis=0, tiled=True)  13.4 us
    all_gather x1, blocking collectives, local(): lax.all_gather(back_gate, 'row', axis=0, tiled=True)  13.3 us
    all_gather x1, blocking collectives, local(): lax.all_gather(back_up, 'row', axis=0, tiled=True)  13.3 us
  transfers between devices with their start and end apart: 14, of which 3 were waited for; matrix products, arithmetic and copies ran while one was open for 3% of the time, Pallas kernels for 0%

commit v1 on v0

v1 whole, which is shorter than its diff:
```python
import jax
import jax.numpy as jnp
from jax import lax
from jax.experimental.layout import Layout, with_layout_constraint
from jax.sharding import PartitionSpec as P

BF16 = jnp.bfloat16
F32 = jnp.float32
NT = (((1,), (1,)), ((), ()))
NN = (((1,), (0,)), ((), ()))
TN = (((0,), (0,)), ((), ()))


def dot(left, right, dims):
    return lax.dot_general(left, right, dims, preferred_element_type=F32)


def row_major(value):
    return with_layout_constraint(value, Layout(major_to_minor=tuple(range(value.ndim))))


def round_up(value, unit):
    return -(-value // unit) * unit


def col_shift(value, step):
    size = lax.axis_size("col")
    return lax.ppermute(value, "col", [(i, (i + step) % size) for i in range(size)])


def parity_groups():
    size = lax.axis_size("col")
    return [list(range(first, size, 2)) for first in range(2)]


def gather_col(block):
    own = lax.all_gather(block, "col", axis=0, tiled=True, axis_index_groups=parity_groups())
    half = own.shape[0] // 2
    low = col_shift(own[:half], 1)
    high = col_shift(own[half:], -1)
    return jnp.concatenate([own, low, high], axis=0)


def scatter_col(parts):
    size = lax.axis_size("col")
    members = size // 2
    rows = parts.shape[0] // size
    width = parts.shape[1]
    count = parts.shape[0] // 2
    half = count // 2
    other = parts[count:].astype(BF16)
    low = col_shift(other[:half], -1)
    high = col_shift(other[half:], 1)
    mine = parts[:count] + jnp.concatenate([low, high], axis=0).astype(F32)
    padded = round_up(rows + 1, 8) - 1
    mine = mine.reshape(members, rows, width)
    mine = jnp.pad(mine, ((0, 0), (0, padded - rows), (0, 0))).reshape(members * padded, width)
    summed = lax.psum_scatter(
        mine, "col", scatter_dimension=0, tiled=True, axis_index_groups=parity_groups()
    )
    return lax.optimization_barrier(summed)[:rows]


def local(tokens, w_gate, w_up, w_down, cotangent, step_rate):
    features = tokens.shape[1]
    hidden_width = w_gate.shape[1]
    n_row = lax.axis_size("row")
    share = hidden_width // n_row
    both = gather_col(jnp.concatenate([tokens, cotangent], axis=1))
    tokens_all = both[:, :features]
    cotangent_all = both[:, features:]
    n_tokens = both.shape[0]

    gate_part = dot(w_gate.T, tokens_all, NT).astype(BF16)
    up_part = dot(w_up.T, tokens_all, NT).astype(BF16)
    back_part = dot(w_down, cotangent_all, NT).astype(BF16)
    parts = jnp.stack(
        [v.reshape(n_row, share, n_tokens) for v in (gate_part, up_part, back_part)], axis=1
    )
    arrived = lax.all_to_all(parts, "row", 0, 0, tiled=True)
    summed = jnp.sum(arrived.astype(F32), axis=0)
    gate_val, up_val, back_hidden = summed[0], summed[1], summed[2]
    gate_sig = jax.nn.sigmoid(gate_val)
    activation = gate_val * gate_sig
    hidden = (activation * up_val).astype(BF16)
    back_gate = (back_hidden * up_val * gate_sig * (1.0 + gate_val * (1.0 - gate_sig))).astype(BF16)
    back_up = (back_hidden * activation).astype(BF16)
    mine = jnp.stack([hidden, back_gate, back_up])
    full = lax.all_to_all(
        jnp.broadcast_to(mine[None], (n_row, *mine.shape)), "row", 0, 0, tiled=True
    )
    hidden_all, gate_grad_all, up_grad_all = (
        full[:, k].reshape(hidden_width, n_tokens) for k in range(3)
    )

    out_part = dot(hidden_all, w_down, TN)
    grad_part = dot(gate_grad_all, w_gate.T, TN) + dot(up_grad_all, w_up.T, TN)
    sums = scatter_col(row_major(jnp.concatenate([out_part, grad_part], axis=1)))
    out_rows = (tokens.astype(F32) + sums[:, :features]).astype(BF16)
    grad_in = (cotangent.astype(F32) + sums[:, features:]).astype(BF16)

    factor = -step_rate[0]
    step_gate = (factor * dot(gate_grad_all, tokens_all, NN)).astype(BF16).T
    step_up = (factor * dot(up_grad_all, tokens_all, NN)).astype(BF16).T
    step_down = (factor * dot(hidden_all, cotangent_all, NN)).astype(BF16)
    return (out_rows, grad_in, step_gate, step_up, step_down)


def solution(mesh):
    in_specs = (
        P(("sweep", "col"), "row"),
        P("row", "col"),
        P("row", "col"),
        P("col", "row"),
        P(("sweep", "col"), "row"),
        P("sweep"),
    )
    out_specs = (
        P(("sweep", "col"), "row"),
        P(("sweep", "col"), "row"),
        P(("sweep", "row"), "col"),
        P(("sweep", "row"), "col"),
        P(("sweep", "col"), "row"),
    )
    return jax.shard_map(local, mesh=mesh, in_specs=in_specs, out_specs=out_specs, check_vma=False)
```

time: 389 us -> 232 us (0.60)
  blocking collectives: 266 us -> 159 us
  starting transfers between devices: 59.9 us -> 18.9 us
  between operations: 15.7 us -> 2.3 us
  waiting for transfers between devices: 28 us -> 33.8 us
    all_gather x5 -> x1, blocking collectives: 195 us -> 79.7 us  [gather_col(): lax.all_gather(block, 'col', axis=0, tiled=True, axis_index_groups=parity...]
    unnamed x12 -> x1, starting transfers between devices: 55.2 us -> 1.31 us
    all_to_all x0 -> x1, blocking collectives: none -> 27.6 us  [local(): arrived = lax.all_to_all(parts, 'row', 0, 0, tiled=True)]
    unnamed x1, blocking collectives: 70.9 us -> 51.8 us
    ppermute x0 -> x4, starting transfers between devices: none -> 13.8 us  [col_shift(): lax.ppermute(value, 'col', [(i, (i + step) % size) for i in range(size)])]
    ppermute x0 -> x4, waiting for transfers between devices: none -> 13.5 us  [col_shift(): lax.ppermute(value, 'col', [(i, (i + step) % size) for i in range(size)])]
    all_to_all x1, waiting for transfers between devices: 26.7 us -> 20.3 us  [local(): lax.all_to_all(jnp.broadcast_to(mine[None], (n_row, *mine.shape)), 'row',...]
    dot_general x6 -> x9, matrix products: 10 us -> 8.29 us  [dot(): return lax.dot_general(left, right, dims, preferred_element_type=F32)]
  transfers between devices with their start and end apart: 14 -> 6, of which waited for: 3 -> 5; matrix products, arithmetic and copies ran while one was open for 3% -> 3% of each run, Pallas kernels for 0% -> 0%
where the time goes in v1:
time: 232 us
  blocking collectives  159 us (69%)
  waiting for transfers between devices  33.8 us (15%)
  starting transfers between devices  18.9 us (8%)
  matrix products  8.29 us (4%)
  local copies, waits for them, and re-layouts  6.88 us (3%)
  other arithmetic  2.38 us (1%)
    all_gather x1, blocking collectives, gather_col(): lax.all_gather(block, 'col', axis=0, tiled=True, axis_index_groups=parity...  79.7 us
    unnamed x1, blocking collectives  51.8 us
    all_to_all x1, blocking collectives, local(): arrived = lax.all_to_all(parts, 'row', 0, 0, tiled=True)  27.6 us
    all_to_all x1, waiting for transfers between devices, local(): lax.all_to_all(jnp.broadcast_to(mine[None], (n_row, *mine.shape)), 'row',...  20.3 us
    ppermute x4, starting transfers between devices, col_shift(): lax.ppermute(value, 'col', [(i, (i + step) % size) for i in range(size)])  13.8 us
    ppermute x4, waiting for transfers between devices, col_shift(): lax.ppermute(value, 'col', [(i, (i + step) % size) for i in range(size)])  13.5 us
    dot_general x9, matrix products, dot(): return lax.dot_general(left, right, dims, preferred_element_type=F32)  8.29 us
  transfers between devices with their start and end apart: 6, of which 5 were waited for; matrix products, arithmetic and copies ran while one was open for 3% of the time, Pallas kernels for 0%

profile of v1, /device:TPU:40, one launch (start us, length us, event | category | flops | bytes accessed | tf_op | source)
XLA Modules:
  0.0 231.6 jit_solution(13161649014903701299)
XLA Ops:
  0.6 0.0 copy-start
  0.6 0.8 maximum_bitcast_fusion
  1.5 79.7 %all-gather = bf16[16,20,1024]{2,1,0:T(8,128)(2,1)S(1)} all-gather(bf16[1,20,1024]{2,1,0:T(8,128)(2,1)S(1)} %maximum_bitcast_fusion), channel_id=1, replica_groups={{0,2,4,6,8,10,12,14,16,18,20,22,24,26,28,30},{1,3,5,7,9,11,13,15,17,19,..., dimensions={0}, use_global_device_ids=true | all-gather | bytes 696320 | tf_op jit(solution)/shard_map/all_gather | solution.py:37
  81.1 0.1 fusion.18
  81.2 0.1 reshape.22
  81.3 5.8 %collective-permute-start = (bf16[160,1024]{1,0:T(8,128)(2,1)S(1)}, bf16[160,1024]{1,0:T(8,128)(2,1)S(1)}, u32[]{:S(2)}, u32[]{:S(2)}) collective-permute-start(bf16[160,1024]{1,0:T(8,128)(2,1)S(1)} %reshape.22), channel_id=1, source_target_pairs={{0,1},{1,2},{2,3},{3,4},{4,5},{5,6},{6,7},{7,8},{8,9},{9,10},{10,1... | collective-permute-start | bytes 983048 | tf_op jit(solution)/shard_map/ppermute | solution.py:28
  87.1 0.1 reshape.23
  87.2 2.0 collective-permute-start.1
  89.1 0.1 reshape.21
  89.2 0.0 copy-start.3
  89.3 2.3 %collective-permute-done = bf16[160,1024]{1,0:T(8,128)(2,1)S(1)} collective-permute-done((bf16[160,1024]{1,0:T(8,128)(2,1)S(1)}, bf16[160,1024]{1,0:T(8,128)(2,1)S(1)}, u32[]{:S(2)}, u32[]{:S(2)}) %collective-permute-start) | collective-permute-done | bytes 327712 | tf_op jit(solution)/shard_map/ppermute | solution.py:28
  91.7 4.5 %collective-permute-done.1 = bf16[160,1024]{1,0:T(8,128)(2,1)S(1)} collective-permute-done((bf16[160,1024]{1,0:T(8,128)(2,1)S(1)}, bf16[160,1024]{1,0:T(8,128)(2,1)S(1)}, u32[]{:S(2)}, u32[]{:S(2)}) %collective-permute-start.1) | collective-permute-done | bytes 327712 | tf_op jit(solution)/shard_map/ppermute | solution.py:28
  96.2 0.0 copy-done.3
  96.2 0.0 copy-start.5
  96.2 0.6 convolution_convert_fusion.1
  96.8 0.0 copy-done
  96.8 0.0 copy-start.4
  96.8 0.6 convolution_convert_fusion
  97.3 0.0 copy-done.5
  97.3 0.4 copy-done.4
  97.8 0.6 convolution_convert_fusion.2
  98.3 0.2 pad_maximum_fusion.1
  98.6 27.6 %all_to_all.10 = bf16[8,3,56,640]{3,2,1,0:T(8,128)(2,1)S(1)} all-to-all(bf16[8,3,56,640]{3,2,1,0:T(8,128)(2,1)S(1)} %pad_maximum_fusion.1), channel_id=1, replica_groups=mesh['sweep'=2,'row'=8,'col'=32] {'row'}, dimensions={0} | all-to-all | bytes 3440640 | tf_op jit(solution)/shard_map/all_to_all | solution.py:80
  126.1 0.2 convert_reduce_fusion
  126.4 0.1 multiply_convert_fusion.2
  126.5 1.3 broadcast_in_dim.2
  127.8 3.8 %all-to-all-start.1 = ((bf16[8,3,56,640]{3,2,1,0:T(8,128)(2,1)}), bf16[8,3,56,640]{3,2,1,0:T(8,128)(2,1)S(1)}, u32[]{:S(2)}, u32[]{:S(2)}) async-start(bf16[8,3,56,640]{3,2,1,0:T(8,128)(2,1)} %broadcast_in_dim.2), calls=%async_computation.1 | async-start | bytes 3440640 | tf_op jit(solution)/shard_map/all_to_all | solution.py:89
  132.3 1.3 dynamic-slice.4
  134.2 20.3 %all-to-all-done.1 = bf16[8,3,56,640]{3,2,1,0:T(8,128)(2,1)S(1)} async-done(((bf16[8,3,56,640]{3,2,1,0:T(8,128)(2,1)}), bf16[8,3,56,640]{3,2,1,0:T(8,128)(2,1)S(1)}, u32[]{:S(2)}, u32[]{:S(2)}) %all-to-all-start.1) | async-done | bytes 1720352 | tf_op jit(solution)/shard_map/all_to_all | solution.py:89
  154.6 0.1 fusion.16
  154.7 0.0 copy-start.1
  154.7 0.5 fusion.19
  155.3 0.5 fusion.20
  155.8 0.0 copy-done.1
  155.8 0.6 convolution_add_fusion
  156.4 0.2 fusion.1
  156.6 0.0 copy-start.6
  156.6 3.3 %collective-permute-start.2 = (bf16[160,1024]{1,0:T(8,128)(2,1)S(1)}, bf16[160,1024]{1,0:T(8,128)(2,1)S(1)}, u32[]{:S(2)}, u32[]{:S(2)}) collective-permute-start(bf16[160,1024]{1,0:T(8,128)(2,1)S(1)} %get-tuple-element.8), channel_id=1, source_target_pairs={{0,31},{1,0},{2,1},{3,2},{4,3},{5,4},{6,5},{7,6},{8,7},{9,8},{10,9... | collective-permute-start | bytes 983048 | tf_op jit(solution)/shard_map/ppermute | solution.py:28
  159.9 2.7 %collective-permute-start.3 = (bf16[160,1024]{1,0:T(8,128)(2,1)S(1)}, bf16[160,1024]{1,0:T(8,128)(2,1)S(1)}, u32[]{:S(2)}, u32[]{:S(2)}) collective-permute-start(bf16[160,1024]{1,0:T(8,128)(2,1)S(1)} %get-tuple-element.9), channel_id=1, source_target_pairs={{0,1},{1,2},{2,3},{3,4},{4,5},{5,6},{6,7},{7,8},{8,9},{9,10},{10,1... | collective-permute-start | bytes 983048 | tf_op jit(solution)/shard_map/ppermute | solution.py:28
  162.7 0.0 copy-done.6
  162.7 1.3 fusion.5
  164.0 1.3 fusion.6
  165.3 2.6 %collective-permute-done.2 = bf16[160,1024]{1,0:T(8,128)(2,1)S(1)} collective-permute-done((bf16[160,1024]{1,0:T(8,128)(2,1)S(1)}, bf16[160,1024]{1,0:T(8,128)(2,1)S(1)}, u32[]{:S(2)}, u32[]{:S(2)}) %collective-permute-start.2) | collective-permute-done | bytes 327712 | tf_op jit(solution)/shard_map/ppermute | solution.py:28
  167.8 4.1 %collective-permute-done.3 = bf16[160,1024]{1,0:T(8,128)(2,1)S(1)} collective-permute-done((bf16[160,1024]{1,0:T(8,128)(2,1)S(1)}, bf16[160,1024]{1,0:T(8,128)(2,1)S(1)}, u32[]{:S(2)}, u32[]{:S(2)}) %collective-permute-start.3) | collective-permute-done | bytes 327712 | tf_op jit(solution)/shard_map/ppermute | solution.py:28
  171.9 0.2 fusion.3
  172.1 1.3 reshape.18
  173.4 1.5 pad.4
  175.0 0.2 reshape.19
  175.2 0.0 copy-start.2
  175.2 51.8 %fusion = f32[24,1024]{1,0:T(8,128)S(1)} fusion(f32[368,1024]{1,0:T(8,128)S(1)} %reshape.19), kind=kCustom, calls=%all-reduce-scatter | all-reduce-scatter fusion | flops 393217 | bytes 1607680
  227.0 0.0 copy-start.7
  227.0 0.0 copy-start.8
  227.0 1.3 collective-permute-start.4
  228.3 0.0 copy-done.2
  228.4 2.4 %fusion.4 = bf16[448,512]{1,0:T(8,128)(2,1)} fusion(bf16[448,640]{1,0:T(8,128)(2,1)S(1)} %bitcast.39, bf16[640,1024]{1,0:T(8,128)(2,1)} %copy-done.5, f32[]{:T(128)} %bitcast.13), kind=kOutput, calls=%fused_computation.15 | convolution fusion | flops 294060032 | bytes 1688064 | tf_op jit(solution)/shard_map/dot_general | solution.py:15
  230.7 0.0 collective-permute-done.4
  230.7 0.2 concatenate.16
  230.9 0.0 copy-done.7
  230.9 0.0 copy-done.8
  230.9 0.6 fusion.14
  (7 shorter events, 0.2 us)
Async XLA Ops:
  0.6 96.1 %copy-start = (bf16[448,512]{1,0:T(8,128)(2,1)S(1)}, bf16[448,512]{1,0:T(8,128)(2,1)}, u32[]{:S(2)}) copy-start(bf16[448,512]{1,0:T(8,128)(2,1)} %param.9) | copy-start | bytes 1376260
  81.3 10.4 %collective-permute-start = (bf16[160,1024]{1,0:T(8,128)(2,1)S(1)}, bf16[160,1024]{1,0:T(8,128)(2,1)S(1)}, u32[]{:S(2)}, u32[]{:S(2)}) collective-permute-start(bf16[160,1024]{1,0:T(8,128)(2,1)S(1)} %reshape.22), channel_id=1, source_target_pairs={{0,1},{1,2},{2,3},{3,4},{4,5},{5,6},{6,7},{7,8},{8,9},{9,10},{10,1... | collective-permute-start | bytes 983048 | tf_op jit(solution)/shard_map/ppermute | solution.py:28
  87.2 9.0 %collective-permute-start.1 = (bf16[160,1024]{1,0:T(8,128)(2,1)S(1)}, bf16[160,1024]{1,0:T(8,128)(2,1)S(1)}, u32[]{:S(2)}, u32[]{:S(2)}) collective-permute-start(bf16[160,1024]{1,0:T(8,128)(2,1)S(1)} %reshape.23), channel_id=1, source_target_pairs={{0,31},{1,0},{2,1},{3,2},{4,3},{5,4},{6,5},{7,6},{8,7},{9,8},{10,9... | collective-permute-start | bytes 983048 | tf_op jit(solution)/shard_map/ppermute | solution.py:28
  89.2 6.9 %copy-start.3 = (bf16[512,448]{0,1:T(8,128)(2,1)S(1)}, bf16[512,448]{0,1:T(8,128)(2,1)}, u32[]{:S(2)}) copy-start(bf16[512,448]{0,1:T(8,128)(2,1)} %param.8) | copy-start | bytes 1376260
  96.2 1.2 copy-start.5
  96.8 1.0 copy-start.4
  127.8 26.7 %all-to-all-start.1 = ((bf16[8,3,56,640]{3,2,1,0:T(8,128)(2,1)}), bf16[8,3,56,640]{3,2,1,0:T(8,128)(2,1)S(1)}, u32[]{:S(2)}, u32[]{:S(2)}) async-start(bf16[8,3,56,640]{3,2,1,0:T(8,128)(2,1)} %broadcast_in_dim.2), calls=%async_computation.1 | async-start | bytes 3440640 | tf_op jit(solution)/shard_map/all_to_all | solution.py:89
  154.7 1.1 copy-start.1
  156.6 6.1 %copy-start.6 = (bf16[640,1024]{1,0:T(8,128)(2,1)S(1)}, bf16[640,1024]{1,0:T(8,128)(2,1)}, u32[]{:S(2)}) copy-start(bf16[640,1024]{1,0:T(8,128)(2,1)} %copy-done.5) | copy-start | bytes 3932164
  156.6 11.2 %collective-permute-start.2 = (bf16[160,1024]{1,0:T(8,128)(2,1)S(1)}, bf16[160,1024]{1,0:T(8,128)(2,1)S(1)}, u32[]{:S(2)}, u32[]{:S(2)}) collective-permute-start(bf16[160,1024]{1,0:T(8,128)(2,1)S(1)} %get-tuple-element.8), channel_id=1, source_target_pairs={{0,31},{1,0},{2,1},{3,2},{4,3},{5,4},{6,5},{7,6},{8,7},{9,8},{10,9... | collective-permute-start | bytes 983048 | tf_op jit(solution)/shard_map/ppermute | solution.py:28
  159.9 12.0 %collective-permute-start.3 = (bf16[160,1024]{1,0:T(8,128)(2,1)S(1)}, bf16[160,1024]{1,0:T(8,128)(2,1)S(1)}, u32[]{:S(2)}, u32[]{:S(2)}) collective-permute-start(bf16[160,1024]{1,0:T(8,128)(2,1)S(1)} %get-tuple-element.9), channel_id=1, source_target_pairs={{0,1},{1,2},{2,3},{3,4},{4,5},{5,6},{6,7},{7,8},{8,9},{9,10},{10,1... | collective-permute-start | bytes 983048 | tf_op jit(solution)/shard_map/ppermute | solution.py:28
  175.2 53.2 %copy-start.2 = (bf16[8,1,56,640]{3,2,1,0:T(8,128)(2,1)S(1)}, bf16[8,1,56,640]{3,2,1,0:T(8,128)(2,1)}, u32[]{:S(2)}) copy-start(bf16[8,1,56,640]{3,2,1,0:T(8,128)(2,1)} %copy-done.1) | copy-start | bytes 1720324
  227.0 3.9 %copy-start.7 = (bf16[20,512]{1,0:T(8,128)(2,1)S(1)}, bf16[20,512]{1,0:T(8,128)(2,1)}, u32[]{:S(2)}) copy-start(bf16[20,512]{1,0:T(8,128)(2,1)} %param.10) | copy-start | bytes 61444
  227.0 3.9 %copy-start.8 = (bf16[20,512]{1,0:T(8,128)(2,1)S(1)}, bf16[20,512]{1,0:T(8,128)(2,1)}, u32[]{:S(2)}) copy-start(bf16[20,512]{1,0:T(8,128)(2,1)} %param.6) | copy-start | bytes 61444
  227.0 3.7 %collective-permute-start.4 = (f32[15,1024]{1,0:T(8,128)S(1)}, f32[15,1024]{1,0:T(8,128)S(1)}, u32[]{:S(2)}, u32[]{:S(2)}) collective-permute-start(f32[15,1024]{1,0:T(8,128)S(1)} %slice.85), channel_id=1, source_target_pairs={{0,2},{2,4},{4,6},{6,8},{8,10},{10,12},{12,14},{14,16},{16,18},{18... | collective-permute-start | bytes 184328

commit v2 on v1

v2 whole, which is shorter than its diff:
```python
import jax
import jax.numpy as jnp
from jax import lax
from jax.experimental.layout import Layout, with_layout_constraint
from jax.sharding import PartitionSpec as P


BF16 = jnp.bfloat16
F32 = jnp.float32
LANES = 128
NT = (((1,), (1,)), ((), ()))
NN = (((1,), (0,)), ((), ()))
TN = (((0,), (0,)), ((), ()))


def dot(left, right, dims):
    return lax.dot_general(left, right, dims, preferred_element_type=F32)


def row_major(value):
    return with_layout_constraint(value, Layout(major_to_minor=tuple(range(value.ndim))))


def round_up(value, unit):
    return -(-value // unit) * unit


def col_shift(value, step):
    size = lax.axis_size("col")
    return lax.ppermute(value, "col", [(i, (i + step) % size) for i in range(size)])


def every_other(axis):
    size = lax.axis_size(axis)
    return [list(range(first, size, 2)) for first in range(2)]


def scatter_col(parts):
    members = lax.axis_size("col") // 2
    rows = parts.shape[0] // members
    width = parts.shape[1]
    padded = round_up(rows + 1, 8) - 1
    parts = parts.reshape(members, rows, width)
    parts = jnp.pad(parts, ((0, 0), (0, padded - rows), (0, 0)))
    parts = parts.reshape(members * padded, width)
    summed = lax.psum_scatter(
        parts, "col", scatter_dimension=0, tiled=True, axis_index_groups=every_other("col")
    )
    return lax.optimization_barrier(summed)[:rows]


def gather_row(block):
    size = lax.axis_size("row")
    mine = lax.all_gather(block, "row", axis=0, axis_index_groups=every_other("row"))
    pair = lax.ppermute(mine, "row", [(i, i ^ 1) for i in range(size)])
    even = lax.axis_index("row") % 2 == 0
    full = jnp.stack([jnp.where(even, mine, pair), jnp.where(even, pair, mine)], axis=1)
    return full.reshape(size * block.shape[0], block.shape[1])


def layer(tokens, w_gate, w_up, w_down, cotangent, step_rate):
    features = tokens.shape[1]
    own = w_gate.shape[1]
    n_row = lax.axis_size("row")
    low = round_up(own // 2, LANES)
    high = own - low
    width = 2 * own
    window = own // LANES * LANES
    extra = own - window

    weights = jnp.stack([w_gate.T, w_up.T, w_down])
    from_below = col_shift(weights[:, low:], 1)
    from_above = col_shift(weights[:, :low], -1)
    block = jnp.concatenate([tokens, cotangent], axis=1)
    both = lax.all_gather(block, "col", axis=0, tiled=True, axis_index_groups=every_other("col"))
    count = both.shape[0]
    half = count // 2
    other = jnp.concatenate(
        [col_shift(both[:half], 1), col_shift(both[half:], -1)],
        axis=0,
    )
    w_gate_t, w_up_t, w_down_t = (
        jnp.concatenate([weights[k], from_below[k], from_above[k]], axis=0) for k in range(3)
    )
    tokens_own, cotangent_own = both[:, :features], both[:, features:]
    tokens_other, cotangent_other = other[:, :features], other[:, features:]

    parts = [
        dot(tokens_own, w_gate_t, NT).astype(BF16),
        dot(tokens_own, w_up_t, NT).astype(BF16),
        dot(cotangent_own, w_down_t, NT).astype(BF16),
    ]
    parts = jnp.concatenate(parts, axis=1)
    parts = parts.reshape(n_row, count // n_row, 3 * width)
    arrived = lax.all_to_all(parts, "row", 0, 0, tiled=True)
    summed = jnp.sum(arrived.astype(F32), axis=0)
    gate_val, up_val, back_hidden = (summed[:, k * width : (k + 1) * width] for k in range(3))
    gate_sig = jax.nn.sigmoid(gate_val)
    activation = gate_val * gate_sig
    hidden = (activation * up_val).astype(BF16)
    back_gate = (back_hidden * up_val * gate_sig * (1.0 + gate_val * (1.0 - gate_sig))).astype(BF16)
    back_up = (back_hidden * activation).astype(BF16)
    full = gather_row(jnp.concatenate([hidden, back_gate, back_up], axis=1))
    parts_of = [full[:, k * width : (k + 1) * width] for k in range(3)]

    to_below = jnp.stack([v[:, window : own + high] for v in parts_of])
    to_above = jnp.stack([v[:, own + high :] for v in parts_of])
    high_other = col_shift(to_below, -1)
    low_other = col_shift(to_above, 1)

    out_part = dot(parts_of[0], w_down_t, NN)
    grad_part = dot(parts_of[1], w_gate_t, NN) + dot(parts_of[2], w_up_t, NN)
    sums = scatter_col(row_major(jnp.concatenate([out_part, grad_part], axis=1)))
    out_rows = (tokens.astype(F32) + sums[:, :features]).astype(BF16)
    grad_in = (cotangent.astype(F32) + sums[:, features:]).astype(BF16)

    factor = -step_rate[0]

    def step(k, rows_own, rows_other):
        mine = dot(parts_of[k][:, :own], rows_own, TN)
        upper = dot(high_other[k], rows_other, TN)[extra:]
        lower = dot(low_other[k], rows_other, TN)
        return (factor * (mine + jnp.concatenate([lower, upper], axis=0))).astype(BF16)

    step_down = step(0, cotangent_own, cotangent_other)
    step_gate = step(1, tokens_own, tokens_other).T
    step_up = step(2, tokens_own, tokens_other).T
    return (out_rows, grad_in, step_gate, step_up, step_down)


def solution(mesh):
    in_specs = (
        P(("sweep", "col"), "row"),
        P("row", "col"),
        P("row", "col"),
        P("col", "row"),
        P(("sweep", "col"), "row"),
        P("sweep"),
    )
    out_specs = (
        P(("sweep", "col"), "row"),
        P(("sweep", "col"), "row"),
        P(("sweep", "row"), "col"),
        P(("sweep", "row"), "col"),
        P(("sweep", "col"), "row"),
    )
    return jax.shard_map(layer, mesh=mesh, in_specs=in_specs, out_specs=out_specs, check_vma=False)
```

time: 232 us -> 266 us (1.15)
  starting transfers between devices: 18.9 us -> 67.2 us
  waiting for transfers between devices: 33.8 us -> 12.1 us
  local copies, waits for them, and re-layouts: 6.88 us -> 14.3 us
  blocking collectives: 159 us -> 153 us
  other arithmetic: 2.38 us -> 6.68 us
    ppermute x4 -> x6, starting transfers between devices: 13.8 us -> 61.8 us  [col_shift(): lax.ppermute(value, 'col', [(i, (i + step) % size) for i in range(size)])]
    all_to_all x1 -> x0, waiting for transfers between devices: 20.3 us -> none  [local(): lax.all_to_all(jnp.broadcast_to(mine[None], (n_row, *mine.shape)), 'row',...]
    all_gather x1 -> x2, blocking collectives: 79.7 us -> 68.7 us  [the longest x1 54.5 us: layer(): lax.all_gather(block, 'col', axis=0, tiled=True, axis_index_groups=every_...]
    unnamed x1, blocking collectives: 51.8 us -> 56.8 us
    all_to_all x1 -> x0, starting transfers between devices: 3.79 us -> none  [local(): lax.all_to_all(jnp.broadcast_to(mine[None], (n_row, *mine.shape)), 'row',...]
    unnamed x25 -> x52, local copies, waits for them, and re-layouts: 2.15 us -> 5.41 us
    another operation x3 -> x5, other arithmetic: 0.41 us -> 3.37 us  [the longest x2 1.5 us: gather_row(): jnp.stack([jnp.where(even, mine, pair), jnp.where(even, pair, mine)], axi...]
    ppermute x4 -> x6, waiting for transfers between devices: 13.5 us -> 12.1 us  [col_shift(): lax.ppermute(value, 'col', [(i, (i + step) % size) for i in range(size)])]
  transfers between devices with their start and end apart: 6 -> 8, of which waited for: 5 -> 3; matrix products, arithmetic and copies ran while one was open for 3% -> 26% of each run, Pallas kernels for 0% -> 0%
where the time goes in v2:
time: 266 us; the launch traced here: 265 us
  blocking collectives  153 us (58%)
  starting transfers between devices  67.2 us (25%)
  local copies, waits for them, and re-layouts  14.3 us (5%)
  waiting for transfers between devices  12.1 us (5%)
  matrix products  8.84 us (3%)
  other arithmetic  6.68 us (3%)
    ppermute x6, starting transfers between devices, col_shift(): lax.ppermute(value, 'col', [(i, (i + step) % size) for i in range(size)])  61.8 us
    unnamed x1, blocking collectives  56.8 us
    all_gather x1, blocking collectives, layer(): lax.all_gather(block, 'col', axis=0, tiled=True, axis_index_groups=every_...  54.5 us
    all_to_all x1, blocking collectives, layer(): arrived = lax.all_to_all(parts, 'row', 0, 0, tiled=True)  27.6 us
    all_gather x1, blocking collectives, gather_row(): lax.all_gather(block, 'row', axis=0, axis_index_groups=every_other('row'))  14.2 us
    ppermute x6, waiting for transfers between devices, col_shift(): lax.ppermute(value, 'col', [(i, (i + step) % size) for i in range(size)])  12.1 us
    dot_general x15, matrix products, dot(): return lax.dot_general(left, right, dims, preferred_element_type=F32)  8.84 us
    unnamed x52, local copies, waits for them, and re-layouts  5.41 us
  transfers between devices with their start and end apart: 8, of which 3 were waited for; matrix products, arithmetic and copies ran while one was open for 26% of the time, Pallas kernels for 0%

profile of v2, /device:TPU:40, one launch (start us, length us, event | category | flops | bytes accessed | tf_op | source)
XLA Modules:
  0.0 264.8 jit_solution(10670530837199976114)
XLA Ops:
  0.7 0.0 copy-start.21
  0.7 2.1 pad_maximum_fusion.8
  2.8 4.7 %collective-permute-start = (bf16[3,192,512]{2,1,0:T(8,128)(2,1)}, bf16[3,192,512]{2,1,0:T(8,128)(2,1)}, u32[]{:S(2)}, u32[]{:S(2)}) collective-permute-start(bf16[3,192,512]{2,1,0:T(8,128)(2,1)} %pad_maximum_fusion.8), channel_id=1, source_target_pairs={{0,1},{1,2},{2,3},{3,4},{4,5},{5,6},{6,7},{7,8},{8,9},{9,10},{10,1... | collective-permute-start | bytes 1769480 | tf_op jit(solution)/shard_map/ppermute | solution.py:30
  7.5 1.0 pad_maximum_fusion.6
  8.5 42.6 %collective-permute-start.1 = (bf16[3,256,512]{2,1,0:T(8,128)(2,1)}, bf16[3,256,512]{2,1,0:T(8,128)(2,1)S(1)}, u32[]{:S(2)}, u32[]{:S(2)}) collective-permute-start(bf16[3,256,512]{2,1,0:T(8,128)(2,1)} %pad_maximum_fusion.6), channel_id=1, source_target_pairs={{0,31},{1,0},{2,1},{3,2},{4,3},{5,4},{6,5},{7,6},{8,7},{9,8},{10,9... | collective-permute-start | bytes 2359304 | tf_op jit(solution)/shard_map/ppermute | solution.py:30
  51.1 54.5 %all-gather.1 = bf16[16,20,1024]{2,1,0:T(8,128)(2,1)S(1)} all-gather(bf16[1,20,1024]{2,1,0:T(8,128)(2,1)S(1)} %maximum_bitcast_fusion), channel_id=1, replica_groups={{0,2,4,6,8,10,12,14,16,18,20,22,24,26,28,30},{1,3,5,7,9,11,13,15,17,19,..., dimensions={0}, use_global_device_ids=true | all-gather | bytes 696320 | tf_op jit(solution)/shard_map/all_gather | solution.py:75
  105.6 1.0 reshape.29
  106.6 1.2 slice_bitcast_fusion.5
  107.8 0.1 slice_bitcast_fusion.2
  107.9 0.0 copy-done.5
  108.0 0.5 convolution_convert_fusion
  108.5 0.2 copy-done.10
  108.7 0.0 copy-done.8
  108.8 0.5 convolution_convert_fusion.2
  109.3 0.5 convolution_convert_fusion.1
  109.9 0.1 pad_maximum_fusion
  110.0 27.6 %all_to_all.5 = bf16[8,40,2688]{2,1,0:T(8,128)(2,1)S(1)} all-to-all(bf16[8,40,2688]{2,1,0:T(8,128)(2,1)S(1)} %bitcast.65), channel_id=1, replica_groups=mesh['sweep'=2,'row'=8,'col'=32] {'row'}, dimensions={0} | all-to-all | bytes 3440640 | tf_op jit(solution)/shard_map/all_to_all | solution.py:95
  137.6 0.2 convert_reduce_fusion
  137.8 0.1 multiply_convert_fusion.2
  137.9 14.2 %all-gather = bf16[160,2688]{1,0:T(8,128)(2,1)S(1)} all-gather(bf16[40,2688]{1,0:T(8,128)(2,1)S(1)} %pad_maximum_fusion.17), channel_id=2, replica_groups={{0,64,128,192},{32,96,160,224},{1,65,129,193},{33,97,161,225},{2,66,130..., dimensions={0}, use_global_device_ids=true | all-gather | bytes 1075200 | tf_op jit(solution)/shard_map/all_gather | solution.py:54
  152.2 1.9 collective-permute-start.2
  154.1 0.8 fusion.56
  154.9 1.1 reshape.30
  156.0 2.0 collective-permute-start.4
  157.9 0.8 reshape.31
  158.7 5.2 %collective-permute-start.5 = (bf16[160,1024]{1,0:T(8,128)(2,1)}, bf16[160,1024]{1,0:T(8,128)(2,1)S(1)}, u32[]{:S(2)}, u32[]{:S(2)}) collective-permute-start(bf16[160,1024]{1,0:T(8,128)(2,1)} %reshape.31), channel_id=1, source_target_pairs={{0,31},{1,0},{2,1},{3,2},{4,3},{5,4},{6,5},{7,6},{8,7},{9,8},{10,9... | collective-permute-start | bytes 983048 | tf_op jit(solution)/shard_map/ppermute | solution.py:30
  164.5 1.3 dynamic-slice.4
  166.5 2.9 %collective-permute-done.4 = bf16[160,1024]{1,0:T(8,128)(2,1)} collective-permute-done((bf16[160,1024]{1,0:T(8,128)(2,1)S(1)}, bf16[160,1024]{1,0:T(8,128)(2,1)}, u32[]{:S(2)}, u32[]{:S(2)}) %collective-permute-start.4) | collective-permute-done | bytes 327712 | tf_op jit(solution)/shard_map/ppermute | solution.py:30
  169.3 1.0 constant_dynamic-update-slice_fusion.1
  170.3 1.2 collective-permute-done.5
  171.6 1.3 select_bitcast_fusion.1
  172.9 0.2 pad_maximum_fusion.1
  173.1 0.7 copy-done.13
  173.8 0.1 copy-done.19
  173.9 0.5 fusion.7
  174.4 0.4 copy-done.11
  174.8 0.1 copy-done.17
  174.9 0.5 fusion.10
  175.4 0.7 slice_bitcast_fusion.20
  176.2 0.2 copy-done.9
  176.4 0.1 copy-done.15
  176.5 0.5 convolution_add_fusion
  177.0 0.1 pad_maximum_fusion.2
  177.1 1.3 reshape.25
  178.4 1.5 pad.4
  179.9 1.3 reshape.26
  181.3 0.1 pad_maximum_fusion.10
  181.3 5.5 %collective-permute-start.6 = (bf16[3,320,256]{2,1,0:T(8,128)(2,1)S(1)}, bf16[3,320,256]{2,1,0:T(8,128)(2,1)S(1)}, u32[]{:S(2)}, u32[]{:S(2)}) collective-permute-start(bf16[3,320,256]{2,1,0:T(8,128)(2,1)S(1)} %pad_maximum_fusion.10), channel_id=1, source_target_pairs={{0,31},{1,0},{2,1},{3,2},{4,3},{5,4},{6,5},{7,6},{8,7},{9,8},{10,9... | collective-permute-start | bytes 1474568 | tf_op jit(solution)/shard_map/ppermute | solution.py:30
  186.9 56.8 %fusion = f32[24,1024]{1,0:T(8,128)S(1)} fusion(f32[368,1024]{1,0:T(8,128)} %reshape.26), kind=kCustom, calls=%all-reduce-scatter | all-reduce-scatter fusion | flops 393217 | bytes 1607680
  243.7 3.5 %collective-permute-start.7 = (f32[15,1024]{1,0:T(8,128)S(1)}, f32[15,1024]{1,0:T(8,128)S(1)}, u32[]{:S(2)}, u32[]{:S(2)}) collective-permute-start(f32[15,1024]{1,0:T(8,128)S(1)} %slice.215), channel_id=1, source_target_pairs={{0,2},{2,4},{4,6},{6,8},{8,10},{10,12},{12,14},{14,16},{16,18},{18... | collective-permute-start | bytes 184328
  247.2 0.9 pad_maximum_fusion.9
  248.1 1.9 collective-permute-start.3
  250.0 0.2 concatenate.44
  250.2 0.6 fusion.48
  250.9 0.4 fusion.26
  251.3 0.4 fusion.32
  251.7 0.4 fusion.36
  252.1 8.1 %collective-permute-done.3 = bf16[3,320,256]{2,1,0:T(8,128)(2,1)S(1)} collective-permute-done((bf16[3,320,256]{2,1,0:T(8,128)(2,1)}, bf16[3,320,256]{2,1,0:T(8,128)(2,1)S(1)}, u32[]{:S(2)}, u32[]{:S(2)}) %collective-permute-start.3) | collective-permute-done | bytes 491552 | tf_op jit(solution)/shard_map/ppermute | solution.py:30
  260.2 0.3 fusion.28
  260.6 1.2 fusion.6
  261.8 0.3 fusion.38
  262.1 1.2 fusion.13
  263.3 0.3 fusion.34
  263.6 1.2 fusion.12
  (47 shorter events, 0.2 us)
Async XLA Ops:
  0.6 6.9 %copy-start.3 = (bf16[448,512]{1,0:T(8,128)(2,1)S(1)}, bf16[448,512]{1,0:T(8,128)(2,1)}, u32[]{:S(2)}) copy-start(bf16[448,512]{1,0:T(8,128)(2,1)} %param.9) | copy-start | bytes 1376260
  0.6 6.9 %copy-start.2 = (bf16[512,448]{0,1:T(8,128)(2,1)S(1)}, bf16[512,448]{0,1:T(8,128)(2,1)}, u32[]{:S(2)}) copy-start(bf16[512,448]{0,1:T(8,128)(2,1)} %param.8) | copy-start | bytes 1376260
  0.7 6.9 %copy-start.4 = (bf16[512,448]{0,1:T(8,128)(2,1)S(1)}, bf16[512,448]{0,1:T(8,128)(2,1)}, u32[]{:S(2)}) copy-start(bf16[512,448]{0,1:T(8,128)(2,1)} %param.7) | copy-start | bytes 1376260
  0.7 50.4 %copy-start.20 = (bf16[20,512]{1,0:T(8,128)(2,1)S(1)}, bf16[20,512]{1,0:T(8,128)(2,1)}, u32[]{:S(2)}) copy-start(bf16[20,512]{1,0:T(8,128)(2,1)} %param.10) | copy-start | bytes 61444
  0.7 50.4 %copy-start.21 = (bf16[20,512]{1,0:T(8,128)(2,1)S(1)}, bf16[20,512]{1,0:T(8,128)(2,1)}, u32[]{:S(2)}) copy-start(bf16[20,512]{1,0:T(8,128)(2,1)} %param.6) | copy-start | bytes 61444
  2.8 103.8 %collective-permute-start = (bf16[3,192,512]{2,1,0:T(8,128)(2,1)}, bf16[3,192,512]{2,1,0:T(8,128)(2,1)}, u32[]{:S(2)}, u32[]{:S(2)}) collective-permute-start(bf16[3,192,512]{2,1,0:T(8,128)(2,1)} %pad_maximum_fusion.8), channel_id=1, source_target_pairs={{0,1},{1,2},{2,3},{3,4},{4,5},{5,6},{6,7},{7,8},{8,9},{9,10},{10,1... | collective-permute-start | bytes 1769480 | tf_op jit(solution)/shard_map/ppermute | solution.py:30
  8.5 99.4 %collective-permute-start.1 = (bf16[3,256,512]{2,1,0:T(8,128)(2,1)}, bf16[3,256,512]{2,1,0:T(8,128)(2,1)S(1)}, u32[]{:S(2)}, u32[]{:S(2)}) collective-permute-start(bf16[3,256,512]{2,1,0:T(8,128)(2,1)} %pad_maximum_fusion.6), channel_id=1, source_target_pairs={{0,31},{1,0},{2,1},{3,2},{4,3},{5,4},{6,5},{7,6},{8,7},{9,8},{10,9... | collective-permute-start | bytes 2359304 | tf_op jit(solution)/shard_map/ppermute | solution.py:30
  106.6 1.4 copy-start.5
  107.8 0.7 copy-start.16
  107.8 0.9 copy-start.14
  107.8 1.5 copy-start.18
  107.9 0.8 copy-start.10
  107.9 0.9 copy-start.8
  107.9 1.4 copy-start.12
  152.2 19.4 %collective-permute-start.2 = (bf16[4,40,2688]{2,1,0:T(8,128)(2,1)S(1)}, bf16[4,40,2688]{2,1,0:T(8,128)(2,1)}, u32[]{:S(2)}, u32[]{:S(2)}) collective-permute-start(bf16[4,40,2688]{2,1,0:T(8,128)(2,1)S(1)} %bitcast.73), channel_id=1, source_target_pairs={{0,32},{32,0},{64,96},{96,64},{128,160},{160,128},{192,224},{224,1... | collective-permute-start | bytes 2580488 | tf_op jit(solution)/shard_map/ppermute | solution.py:55
  156.0 13.4 %collective-permute-start.4 = (bf16[160,1024]{1,0:T(8,128)(2,1)S(1)}, bf16[160,1024]{1,0:T(8,128)(2,1)}, u32[]{:S(2)}, u32[]{:S(2)}) collective-permute-start(bf16[160,1024]{1,0:T(8,128)(2,1)S(1)} %reshape.30), channel_id=1, source_target_pairs={{0,1},{1,2},{2,3},{3,4},{4,5},{5,6},{6,7},{7,8},{8,9},{9,10},{10,1... | collective-permute-start | bytes 983048 | tf_op jit(solution)/shard_map/ppermute | solution.py:30
  158.7 12.8 %collective-permute-start.5 = (bf16[160,1024]{1,0:T(8,128)(2,1)}, bf16[160,1024]{1,0:T(8,128)(2,1)S(1)}, u32[]{:S(2)}, u32[]{:S(2)}) collective-permute-start(bf16[160,1024]{1,0:T(8,128)(2,1)} %reshape.31), channel_id=1, source_target_pairs={{0,31},{1,0},{2,1},{3,2},{4,3},{5,4},{6,5},{7,6},{8,7},{9,8},{10,9... | collective-permute-start | bytes 983048 | tf_op jit(solution)/shard_map/ppermute | solution.py:30
  172.9 1.0 copy-start.13
  172.9 1.0 copy-start.19
  173.1 3.1 %copy-start = (bf16[4,2,40,2688]{3,2,1,0:T(8,128)(2,1)}, bf16[4,2,40,2688]{3,2,1,0:T(8,128)(2,1)S(1)}, u32[]{:S(2)}) copy-start(bf16[4,2,40,2688]{3,2,1,0:T(8,128)(2,1)S(1)} %pad_maximum_fusion.1) | copy-start | bytes 5160964
  173.9 0.9 copy-start.11
  173.9 1.0 copy-start.17
  175.4 1.0 copy-start.9
  175.4 1.1 copy-start.15
  179.9 1.3 copy-start.7
  181.3 68.9 %copy-start.22 = (bf16[20,512]{1,0:T(8,128)(2,1)S(1)}, bf16[20,512]{1,0:T(8,128)(2,1)}, u32[]{:S(2)}) copy-start(bf16[20,512]{1,0:T(8,128)(2,1)} %param.6) | copy-start | bytes 61444
  181.3 69.5 %collective-permute-start.6 = (bf16[3,320,256]{2,1,0:T(8,128)(2,1)S(1)}, bf16[3,320,256]{2,1,0:T(8,128)(2,1)S(1)}, u32[]{:S(2)}, u32[]{:S(2)}) collective-permute-start(bf16[3,320,256]{2,1,0:T(8,128)(2,1)S(1)} %pad_maximum_fusion.10), channel_id=1, source_target_pairs={{0,31},{1,0},{2,1},{3,2},{4,3},{5,4},{6,5},{7,6},{8,7},{9,8},{10,9... | collective-permute-start | bytes 1474568 | tf_op jit(solution)/shard_map/ppermute | solution.py:30
  243.7 6.3 %collective-permute-start.7 = (f32[15,1024]{1,0:T(8,128)S(1)}, f32[15,1024]{1,0:T(8,128)S(1)}, u32[]{:S(2)}, u32[]{:S(2)}) collective-permute-start(f32[15,1024]{1,0:T(8,128)S(1)} %slice.215), channel_id=1, source_target_pairs={{0,2},{2,4},{4,6},{6,8},{8,10},{10,12},{12,14},{14,16},{16,18},{18... | collective-permute-start | bytes 184328
  248.1 12.2 %collective-permute-start.3 = (bf16[3,320,256]{2,1,0:T(8,128)(2,1)}, bf16[3,320,256]{2,1,0:T(8,128)(2,1)S(1)}, u32[]{:S(2)}, u32[]{:S(2)}) collective-permute-start(bf16[3,320,256]{2,1,0:T(8,128)(2,1)} %pad_maximum_fusion.9), channel_id=1, source_target_pairs={{0,1},{1,2},{2,3},{3,4},{4,5},{5,6},{6,7},{7,8},{8,9},{9,10},{10,1... | collective-permute-start | bytes 1474568 | tf_op jit(solution)/shard_map/ppermute | solution.py:30
  250.9 9.6 %copy-start.1 = (bf16[4,2,40,2688]{3,2,1,0:T(8,128)(2,1)S(1)}, bf16[4,2,40,2688]{3,2,1,0:T(8,128)(2,1)}, u32[]{:S(2)}) copy-start(bf16[4,2,40,2688]{3,2,1,0:T(8,128)(2,1)} %copy-done) | copy-start | bytes 5160964
  250.9 9.6 %copy-start.6 = (bf16[320,1024]{1,0:T(8,128)(2,1)S(1)}, bf16[320,1024]{1,0:T(8,128)(2,1)}, u32[]{:S(2)}) copy-start(bf16[320,1024]{1,0:T(8,128)(2,1)} %reshape.29) | copy-start | bytes 1966084

commit v3 on v2

v3 whole, which is shorter than its diff:
```python
import jax
import jax.numpy as jnp
from jax import lax
from jax.experimental.layout import Layout, with_layout_constraint
from jax.sharding import PartitionSpec as P

BF16 = jnp.bfloat16
F32 = jnp.float32
NT = (((1,), (1,)), ((), ()))
NN = (((1,), (0,)), ((), ()))
TN = (((0,), (0,)), ((), ()))


def dot(left, right, dims):
    return lax.dot_general(left, right, dims, preferred_element_type=F32)


def row_major(value):
    return with_layout_constraint(value, Layout(major_to_minor=tuple(range(value.ndim))))


def round_up(value, unit):
    return -(-value // unit) * unit


def every_other(axis):
    size = lax.axis_size(axis)
    return [list(range(first, size, 2)) for first in range(2)]


def move(value, swap, step):
    rows, cols = lax.axis_size("row"), lax.axis_size("col")
    pairs = []
    for row in range(rows):
        for col in range(cols):
            to_row = row ^ 1 if swap else row
            to_col = (col + (step if row % 2 == 0 else -step)) % cols
            pairs.append((row * cols + col, to_row * cols + to_col))
    return lax.ppermute(value, ("row", "col"), pairs)


def gather_col(block):
    return lax.all_gather(block, "col", axis=0, tiled=True, axis_index_groups=every_other("col"))


def scatter_col(parts):
    members = lax.axis_size("col") // 2
    rows = parts.shape[0] // members
    width = parts.shape[1]
    padded = round_up(rows + 1, 8) - 1
    parts = parts.reshape(members, rows, width)
    parts = jnp.pad(parts, ((0, 0), (0, padded - rows), (0, 0))).reshape(members * padded, width)
    summed = lax.psum_scatter(
        parts, "col", scatter_dimension=0, tiled=True, axis_index_groups=every_other("col")
    )
    return lax.optimization_barrier(summed)[:rows]


def layer(tokens, w_gate, w_up, w_down, cotangent, step_rate):
    features = tokens.shape[1]
    own = w_gate.shape[1]
    core = lax.axis_index("row") % 2
    first = core == 0
    weights = jnp.concatenate([w_gate.T, w_up.T, w_down], axis=0)

    gathered = gather_col(jnp.concatenate([tokens, cotangent], axis=1))
    count = gathered.shape[0]
    half = count // 2
    same = lax.dynamic_slice_in_dim(gathered, core * half, half)
    cross = lax.dynamic_slice_in_dim(gathered, (1 - core) * half, half)
    rows_own = jnp.concatenate([same, move(same, False, 1)], axis=0)
    rows_pair = jnp.concatenate([move(cross, True, 0), move(cross, True, -1)], axis=0)
    weights_pair = move(weights, True, 0)

    wide = 2 * own
    tall = 3 * own
    both_part = dot(rows_own[:, :features], weights[:wide], NT) + dot(
        rows_pair[:, :features], weights_pair[:wide], NT
    )
    back_part = dot(rows_own[:, features:], weights[wide:], NT) + dot(
        rows_pair[:, features:], weights_pair[wide:], NT
    )
    parts = jnp.concatenate([both_part.astype(BF16), back_part.astype(BF16)], axis=1)
    members = lax.axis_size("row") // 2
    arrived = lax.all_to_all(
        parts.reshape(members, count // members, tall),
        "row",
        0,
        0,
        axis_index_groups=every_other("row"),
        tiled=True,
    )
    summed = jnp.sum(arrived.astype(F32), axis=0)
    gate_val, up_val, back_hidden = (summed[:, k * own : (k + 1) * own] for k in range(3))
    gate_sig = jax.nn.sigmoid(gate_val)
    activation = gate_val * gate_sig
    hidden = (activation * up_val).astype(BF16)
    back_gate = (back_hidden * up_val * gate_sig * (1.0 + gate_val * (1.0 - gate_sig))).astype(BF16)
    back_up = (back_hidden * activation).astype(BF16)
    acts = lax.all_gather(
        jnp.concatenate([back_gate, back_up, hidden], axis=1),
        "row",
        axis=0,
        tiled=True,
        axis_index_groups=every_other("row"),
    )

    def outputs(matrix):
        return row_major(
            jnp.concatenate(
                [dot(acts[:, wide:], matrix[wide:], NN), dot(acts[:, :wide], matrix[:wide], NN)],
                axis=1,
            )
        )

    out_pair = outputs(weights_pair).astype(BF16)
    out_own = outputs(weights)
    far = move(out_pair[half:], True, -1)
    near = move(out_own[half:].astype(BF16), False, -1)
    pair = move(out_pair[:half], True, 0)
    sum_same = out_own[:half] + near.astype(F32)
    sum_cross = pair.astype(F32) + far.astype(F32)
    sums = scatter_col(
        jnp.concatenate(
            [jnp.where(first, sum_same, sum_cross), jnp.where(first, sum_cross, sum_same)], axis=0
        )
    )
    out_rows = (tokens.astype(F32) + sums[:, :features]).astype(BF16)
    grad_in = (cotangent.astype(F32) + sums[:, features:]).astype(BF16)

    acts_pair = move(acts, True, 0)
    rows_rest = move(rows_pair, True, 0)
    factor = -step_rate[0]
    steps_in = dot(acts[:, :wide], rows_own[:, :features], TN) + dot(
        acts_pair[:, :wide], rows_rest[:, :features], TN
    )
    steps_out = dot(acts[:, wide:], rows_own[:, features:], TN) + dot(
        acts_pair[:, wide:], rows_rest[:, features:], TN
    )
    steps_in = (factor * steps_in).astype(BF16)
    step_down = (factor * steps_out).astype(BF16)
    return (out_rows, grad_in, steps_in[:own].T, steps_in[own:].T, step_down)


def solution(mesh):
    in_specs = (
        P(("sweep", "col"), "row"),
        P("row", "col"),
        P("row", "col"),
        P("col", "row"),
        P(("sweep", "col"), "row"),
        P("sweep"),
    )
    out_specs = (
        P(("sweep", "col"), "row"),
        P(("sweep", "col"), "row"),
        P(("sweep", "row"), "col"),
        P(("sweep", "row"), "col"),
        P(("sweep", "col"), "row"),
    )
    return jax.shard_map(layer, mesh=mesh, in_specs=in_specs, out_specs=out_specs, check_vma=False)
```

time: 266 us -> 227 us (0.85)
  starting transfers between devices: 67.2 us -> 24.4 us
  blocking collectives: 153 us -> 164 us
  matrix products: 8.84 us -> 17.7 us
  local copies, waits for them, and re-layouts: 14.3 us -> 5.71 us
  waiting for transfers between devices: 12.1 us -> 8.16 us
  other arithmetic: 6.68 us -> 3.76 us
    ppermute x7 -> x9, starting transfers between devices: 63.8 us -> 20.2 us  [move(): return lax.ppermute(value, ('row', 'col'), pairs)]
    all_gather x2, blocking collectives: 68.7 us -> 95.2 us  [the longest x1 80.2 us: gather_col(): lax.all_gather(block, 'col', axis=0, tiled=True, axis_index_groups=every_...]
    dot_general x15 -> x12, matrix products: 8.84 us -> 17.7 us  [dot(): return lax.dot_general(left, right, dims, preferred_element_type=F32)]
    all_to_all x1, blocking collectives: 27.6 us -> 18.8 us  [layer(): lax.all_to_all(parts.reshape(members, count // members, tall), 'row', 0,...]
    unnamed x1, blocking collectives: 56.8 us -> 50.4 us
    ppermute x7 -> x9, waiting for transfers between devices: 12.1 us -> 8.16 us  [move(): return lax.ppermute(value, ('row', 'col'), pairs)]
    another operation x5 -> x1, other arithmetic: 3.37 us -> 0.04 us  [the longest x2 1.5 us: gather_row(): jnp.stack([jnp.where(even, mine, pair), jnp.where(even, pair, mine)], axi...]
    unnamed x52 -> x24, local copies, waits for them, and re-layouts: 5.41 us -> 3.27 us
  transfers between devices with their start and end apart: 8 -> 10, of which waited for: 3 -> 3; matrix products, arithmetic and copies ran while one was open for 26% -> 26% of each run, Pallas kernels for 0% -> 0%
where the time goes in v3:
time: 227 us
  blocking collectives  164 us (72%)
  starting transfers between devices  24.4 us (11%)
  matrix products  17.7 us (8%)
  waiting for transfers between devices  8.16 us (4%)
  local copies, waits for them, and re-layouts  5.71 us (3%)
  other arithmetic  3.76 us (2%)
  between operations  2.4 us (1%)
    all_gather x1, blocking collectives, gather_col(): lax.all_gather(block, 'col', axis=0, tiled=True, axis_index_groups=every_...  80.2 us
    unnamed x1, blocking collectives  50.4 us
    ppermute x9, starting transfers between devices, move(): return lax.ppermute(value, ('row', 'col'), pairs)  20.2 us
    all_to_all x1, blocking collectives, layer(): lax.all_to_all(parts.reshape(members, count // members, tall), 'row', 0,...  18.8 us
    dot_general x12, matrix products, dot(): return lax.dot_general(left, right, dims, preferred_element_type=F32)  17.7 us
    all_gather x1, blocking collectives, layer(): lax.all_gather(jnp.concatenate([back_gate, back_up, hidden], axis=1), 'ro...  15 us
    ppermute x9, waiting for transfers between devices, move(): return lax.ppermute(value, ('row', 'col'), pairs)  8.16 us
  transfers between devices with their start and end apart: 10, of which 3 were waited for; matrix products, arithmetic and copies ran while one was open for 26% of the time, Pallas kernels for 0%

profile of v3, /device:TPU:40, one launch (start us, length us, event | category | flops | bytes accessed | tf_op | source)
XLA Modules:
  0.0 226.5 jit_solution(5878789375793929931)
XLA Ops:
  0.7 1.4 pad_maximum_fusion
  2.0 2.0 collective-permute-start.3
  4.1 80.2 %all-gather = bf16[16,20,1024]{2,1,0:T(8,128)(2,1)S(1)} all-gather(bf16[1,20,1024]{2,1,0:T(8,128)(2,1)S(1)} %maximum_bitcast_fusion), channel_id=1, replica_groups={{0,2,4,6,8,10,12,14,16,18,20,22,24,26,28,30},{1,3,5,7,9,11,13,15,17,19,..., dimensions={0}, use_global_device_ids=true | all-gather | bytes 696320 | tf_op jit(solution)/shard_map/all_gather | solution.py:43
  84.3 0.1 reshape.24
  84.5 0.1 constant_dynamic-slice_fusion.2
  84.5 2.0 collective-permute-start.1
  86.5 2.0 collective-permute-start.2
  88.4 4.1 %collective-permute-start = (bf16[160,1024]{1,0:T(8,128)(2,1)S(1)}, bf16[160,1024]{1,0:T(8,128)(2,1)S(1)}, u32[]{:S(2)}, u32[]{:S(2)}) collective-permute-start(bf16[160,1024]{1,0:T(8,128)(2,1)S(1)} %get-tuple-element.11), channel_id=1, source_target_pairs={{0,1},{1,2},{2,3},{3,4},{4,5},{5,6},{6,7},{7,8},{8,9},{9,10},{10,1... | collective-permute-start | bytes 983048 | tf_op jit(solution)/shard_map/ppermute | solution.py:39
  92.5 0.0 collective-permute-done.1
  92.5 0.8 constant_dynamic-update-slice_fusion.1
  93.3 3.8 %collective-permute-done.2 = bf16[160,1024]{1,0:T(8,128)(2,1)S(1)} collective-permute-done((bf16[160,1024]{1,0:T(8,128)(2,1)S(1)}, bf16[160,1024]{1,0:T(8,128)(2,1)S(1)}, u32[]{:S(2)}, u32[]{:S(2)}) %collective-permute-start.2) | collective-permute-done | bytes 327712 | tf_op jit(solution)/shard_map/ppermute | solution.py:39
  97.1 0.7 constant_dynamic-update-slice_fusion
  97.8 0.0 collective-permute-done.3
  97.8 1.5 fusion.22
  99.3 0.0 copy-start
  99.3 1.9 fusion.7
  101.2 0.0 copy-start.3
  101.2 0.0 copy-start.5
  101.2 0.0 collective-permute-done
  101.2 0.0 copy-start.1
  101.2 0.4 fusion.4
  101.6 0.4 copy-done.1
  102.0 0.4 copy-done.3
  102.3 0.1 copy-done.5
  102.5 0.5 fusion.2
  103.0 0.1 pad_maximum_fusion.3
  103.1 18.8 %all_to_all.5 = bf16[4,80,1344]{2,1,0:T(8,128)(2,1)S(1)} all-to-all(bf16[4,80,1344]{2,1,0:T(8,128)(2,1)S(1)} %bitcast.15), channel_id=1, replica_groups={{0,64,128,192},{32,96,160,224},{1,65,129,193},{33,97,161,225},{2,66,130..., dimensions={0} | all-to-all | bytes 1720320 | tf_op jit(solution)/shard_map/all_to_all | solution.py:85
  121.9 0.1 convert_reduce_fusion
  122.0 0.0 copy-start.4
  122.0 0.0 copy-start.6
  122.0 0.1 multiply_convert_fusion.1
  122.2 0.1 concatenate.36
  122.3 15.0 %all_gather.7 = bf16[320,1344]{1,0:T(8,128)(2,1)} all-gather(bf16[80,1344]{1,0:T(8,128)(2,1)S(1)} %concatenate.36), channel_id=1, replica_groups={{0,64,128,192},{32,96,160,224},{1,65,129,193},{33,97,161,225},{2,66,130..., dimensions={0}, use_global_device_ids=true | all-gather | bytes 1075200 | tf_op jit(solution)/shard_map/all_gather | solution.py:100
  137.3 1.6 fusion.14
  138.8 1.3 fusion.33
  140.1 1.4 fusion.20
  141.6 1.9 fusion.5
  143.4 0.1 maximum_convert_fusion
  143.6 2.0 collective-permute-start.5
  145.5 2.0 collective-permute-start.6
  147.5 2.0 collective-permute-start.4
  149.5 2.4 %collective-permute-start.8 = (bf16[320,1024]{1,0:T(8,128)(2,1)}, bf16[320,1024]{1,0:T(8,128)(2,1)}, u32[]{:S(2)}, u32[]{:S(2)}) collective-permute-start(bf16[320,1024]{1,0:T(8,128)(2,1)} %constant_dynamic-update-slice_fusion), channel_id=1, source_target_pairs={{0,32},{1,33},{2,34},{3,35},{4,36},{5,37},{6,38},{7,39},{8,40},{9,... | collective-permute-start | bytes 1966088 | tf_op jit(solution)/shard_map/ppermute | solution.py:39
  152.0 2.0 collective-permute-start.7
  153.9 0.0 collective-permute-done.5
  153.9 1.2 collective-permute-done.6
  155.2 3.1 %collective-permute-done.4 = bf16[160,1024]{1,0:T(8,128)(2,1)} collective-permute-done((bf16[160,1024]{1,0:T(8,128)(2,1)S(1)}, bf16[160,1024]{1,0:T(8,128)(2,1)}, u32[]{:S(2)}, u32[]{:S(2)}) %collective-permute-start.4) | collective-permute-done | bytes 327712 | tf_op jit(solution)/shard_map/ppermute | solution.py:39
  158.3 1.2 fusion.13
  159.4 0.1 pad_maximum_fusion.1
  159.6 0.1 reshape.21
  159.7 0.2 pad.4
  159.9 0.2 reshape.22
  160.1 50.4 %fusion = f32[24,1024]{1,0:T(8,128)S(1)} fusion(f32[368,1024]{1,0:T(8,128)S(1)} %reshape.22), kind=kCustom, calls=%all-reduce-scatter | all-reduce-scatter fusion | flops 393217 | bytes 1607680
  210.6 4.3 %collective-permute-start.9 = (f32[15,1024]{1,0:T(8,128)S(1)}, f32[15,1024]{1,0:T(8,128)S(1)}, u32[]{:S(2)}, u32[]{:S(2)}) collective-permute-start(f32[15,1024]{1,0:T(8,128)S(1)} %slice.130), channel_id=1, source_target_pairs={{0,2},{2,4},{4,6},{6,8},{8,10},{10,12},{12,14},{14,16},{16,18},{18... | collective-permute-start | bytes 184328
  215.5 1.3 dynamic-slice.4
  217.4 0.0 collective-permute-done.9
  217.4 0.2 concatenate.40
  217.6 0.6 fusion.36
  218.2 0.0 collective-permute-done.8
  218.2 0.0 collective-permute-done.7
  218.2 1.9 fusion.15
  220.1 1.7 multiply_convert_fusion
  221.9 1.0 slice_bitcast_fusion
  222.8 1.5 fusion.25
  224.3 2.2 fusion.3
  (14 shorter events, 0.1 us)
Async XLA Ops:
  0.6 3.4 %copy-start.7 = (bf16[20,512]{1,0:T(8,128)(2,1)S(1)}, bf16[20,512]{1,0:T(8,128)(2,1)}, u32[]{:S(2)}) copy-start(bf16[20,512]{1,0:T(8,128)(2,1)} %param.10) | copy-start | bytes 61444
  0.6 3.4 %copy-start.8 = (bf16[20,512]{1,0:T(8,128)(2,1)S(1)}, bf16[20,512]{1,0:T(8,128)(2,1)}, u32[]{:S(2)}) copy-start(bf16[20,512]{1,0:T(8,128)(2,1)} %param.6) | copy-start | bytes 61444
  2.0 95.8 %collective-permute-start.3 = (bf16[1344,512]{1,0:T(8,128)(2,1)S(1)}, bf16[1344,512]{1,0:T(8,128)(2,1)}, u32[]{:S(2)}, u32[]{:S(2)}) collective-permute-start(bf16[1344,512]{1,0:T(8,128)(2,1)S(1)} %pad_maximum_fusion), channel_id=1, source_target_pairs={{0,32},{1,33},{2,34},{3,35},{4,36},{5,37},{6,38},{7,39},{8,40},{9,... | collective-permute-start | bytes 4128776 | tf_op jit(solution)/shard_map/ppermute | solution.py:39
  84.5 8.0 %collective-permute-start.1 = (bf16[160,1024]{1,0:T(8,128)(2,1)S(1)}, bf16[160,1024]{1,0:T(8,128)(2,1)S(1)}, u32[]{:S(2)}, u32[]{:S(2)}) collective-permute-start(bf16[160,1024]{1,0:T(8,128)(2,1)S(1)} %get-tuple-element.12), channel_id=1, source_target_pairs={{0,32},{1,33},{2,34},{3,35},{4,36},{5,37},{6,38},{7,39},{8,40},{9,... | collective-permute-start | bytes 983048 | tf_op jit(solution)/shard_map/ppermute | solution.py:39
  86.5 10.6 %collective-permute-start.2 = (bf16[160,1024]{1,0:T(8,128)(2,1)S(1)}, bf16[160,1024]{1,0:T(8,128)(2,1)S(1)}, u32[]{:S(2)}, u32[]{:S(2)}) collective-permute-start(bf16[160,1024]{1,0:T(8,128)(2,1)S(1)} %get-tuple-element.12), channel_id=1, source_target_pairs={{0,63},{1,32},{2,33},{3,34},{4,35},{5,36},{6,37},{7,38},{8,39},{9,... | collective-permute-start | bytes 983048 | tf_op jit(solution)/shard_map/ppermute | solution.py:39
  88.4 12.8 %collective-permute-start = (bf16[160,1024]{1,0:T(8,128)(2,1)S(1)}, bf16[160,1024]{1,0:T(8,128)(2,1)S(1)}, u32[]{:S(2)}, u32[]{:S(2)}) collective-permute-start(bf16[160,1024]{1,0:T(8,128)(2,1)S(1)} %get-tuple-element.11), channel_id=1, source_target_pairs={{0,1},{1,2},{2,3},{3,4},{4,5},{5,6},{6,7},{7,8},{8,9},{9,10},{10,1... | collective-permute-start | bytes 983048 | tf_op jit(solution)/shard_map/ppermute | solution.py:39
  99.3 1.9 copy-start
  101.2 1.1 copy-start.3
  101.2 1.3 copy-start.5
  101.2 0.7 copy-start.1
  122.0 15.2 %copy-start.4 = (bf16[512,448]{0,1:T(8,128)(2,1)S(1)}, bf16[512,448]{0,1:T(8,128)(2,1)}, u32[]{:S(2)}) copy-start(bf16[512,448]{0,1:T(8,128)(2,1)} %param.8) | copy-start | bytes 1376260
  122.0 15.2 %copy-start.6 = (bf16[512,448]{0,1:T(8,128)(2,1)S(1)}, bf16[512,448]{0,1:T(8,128)(2,1)}, u32[]{:S(2)}) copy-start(bf16[512,448]{0,1:T(8,128)(2,1)} %param.7) | copy-start | bytes 1376260
  143.6 10.3 %collective-permute-start.5 = (bf16[160,1024]{1,0:T(8,128)(2,1)S(1)}, bf16[160,1024]{1,0:T(8,128)(2,1)S(1)}, u32[]{:S(2)}, u32[]{:S(2)}) collective-permute-start(bf16[160,1024]{1,0:T(8,128)(2,1)S(1)} %get-tuple-element.9), channel_id=1, source_target_pairs={{0,32},{1,33},{2,34},{3,35},{4,36},{5,37},{6,38},{7,39},{8,40},{9,... | collective-permute-start | bytes 983048 | tf_op jit(solution)/shard_map/ppermute | solution.py:39
  145.5 9.6 %collective-permute-start.6 = (bf16[160,1024]{1,0:T(8,128)(2,1)S(1)}, bf16[160,1024]{1,0:T(8,128)(2,1)S(1)}, u32[]{:S(2)}, u32[]{:S(2)}) collective-permute-start(bf16[160,1024]{1,0:T(8,128)(2,1)S(1)} %get-tuple-element.10), channel_id=1, source_target_pairs={{0,63},{1,32},{2,33},{3,34},{4,35},{5,36},{6,37},{7,38},{8,39},{9,... | collective-permute-start | bytes 983048 | tf_op jit(solution)/shard_map/ppermute | solution.py:39
  147.5 10.7 %collective-permute-start.4 = (bf16[160,1024]{1,0:T(8,128)(2,1)S(1)}, bf16[160,1024]{1,0:T(8,128)(2,1)}, u32[]{:S(2)}, u32[]{:S(2)}) collective-permute-start(bf16[160,1024]{1,0:T(8,128)(2,1)S(1)} %fusion.11), channel_id=1, source_target_pairs={{0,31},{1,0},{2,1},{3,2},{4,3},{5,4},{6,5},{7,6},{8,7},{9,8},{10,9... | collective-permute-start | bytes 983048 | tf_op jit(solution)/shard_map/ppermute | solution.py:39
  149.5 68.7 %collective-permute-start.8 = (bf16[320,1024]{1,0:T(8,128)(2,1)}, bf16[320,1024]{1,0:T(8,128)(2,1)}, u32[]{:S(2)}, u32[]{:S(2)}) collective-permute-start(bf16[320,1024]{1,0:T(8,128)(2,1)} %constant_dynamic-update-slice_fusion), channel_id=1, source_target_pairs={{0,32},{1,33},{2,34},{3,35},{4,36},{5,37},{6,38},{7,39},{8,40},{9,... | collective-permute-start | bytes 1966088 | tf_op jit(solution)/shard_map/ppermute | solution.py:39
  152.0 66.3 %collective-permute-start.7 = (bf16[320,1344]{1,0:T(8,128)(2,1)}, bf16[320,1344]{1,0:T(8,128)(2,1)}, u32[]{:S(2)}, u32[]{:S(2)}) collective-permute-start(bf16[320,1344]{1,0:T(8,128)(2,1)} %all_gather.7), channel_id=1, source_target_pairs={{0,32},{1,33},{2,34},{3,35},{4,36},{5,37},{6,38},{7,39},{8,40},{9,... | collective-permute-start | bytes 2580488 | tf_op jit(solution)/shard_map/ppermute | solution.py:39
  210.6 6.8 %collective-permute-start.9 = (f32[15,1024]{1,0:T(8,128)S(1)}, f32[15,1024]{1,0:T(8,128)S(1)}, u32[]{:S(2)}, u32[]{:S(2)}) collective-permute-start(f32[15,1024]{1,0:T(8,128)S(1)} %slice.130), channel_id=1, source_target_pairs={{0,2},{2,4},{4,6},{6,8},{8,10},{10,12},{12,14},{14,16},{16,18},{18... | collective-permute-start | bytes 184328
  218.2 1.9 copy-start.2

commit v4 on v3

--- a/solution.py
+++ b/solution.py
@@ -3,6 +3,7 @@
 from jax import lax
 from jax.experimental.layout import Layout, with_layout_constraint
 from jax.sharding import PartitionSpec as P
+
 
 BF16 = jnp.bfloat16
 F32 = jnp.float32
@@ -61,13 +62,15 @@
     own = w_gate.shape[1]
     core = lax.axis_index("row") % 2
     first = core == 0
-    weights = jnp.concatenate([w_gate.T, w_up.T, w_down], axis=0)
-
     gathered = gather_col(jnp.concatenate([tokens, cotangent], axis=1))
     count = gathered.shape[0]
     half = count // 2
     same = lax.dynamic_slice_in_dim(gathered, core * half, half)
     cross = lax.dynamic_slice_in_dim(gathered, (1 - core) * half, half)
+    same, cross, w_gate, w_up, w_down = lax.optimization_barrier(
+        (same, cross, w_gate, w_up, w_down)
+    )
+    weights = jnp.concatenate([w_gate.T, w_up.T, w_down], axis=0)
     rows_own = jnp.concatenate([same, move(same, False, 1)], axis=0)
     rows_pair = jnp.concatenate([move(cross, True, 0), move(cross, True, -1)], axis=0)
     weights_pair = move(weights, True, 0)
@@ -115,9 +118,22 @@
 
     out_pair = outputs(weights_pair).astype(BF16)
     out_own = outputs(weights)
-    far = move(out_pair[half:], True, -1)
-    near = move(out_own[half:].astype(BF16), False, -1)
-    pair = move(out_pair[:half], True, 0)
+    far, near, pair = out_pair[half:], out_own[half:].astype(BF16), out_pair[:half]
+    far, near, pair, held = lax.optimization_barrier((far, near, pair, acts))
+    far = move(far, True, -1)
+    near = move(near, False, -1)
+    pair = move(pair, True, 0)
+
+    def partial_steps(rows):
+        return [
+            dot(held[:, :wide], rows[:, :features], TN),
+            dot(held[:, wide:], rows[:, features:], TN),
+        ]
+
+    steps_rest = [value.astype(BF16) for value in partial_steps(rows_pair)]
+    steps_rest = move(jnp.concatenate(steps_rest, axis=0), True, 0)
+    in_own, out_own_steps = lax.optimization_barrier(partial_steps(rows_own))
+
     sum_same = out_own[:half] + near.astype(F32)
     sum_cross = pair.astype(F32) + far.astype(F32)
     sums = scatter_col(
@@ -125,21 +141,22 @@
             [jnp.where(first, sum_same, sum_cross), jnp.where(first, sum_cross, sum_same)], axis=0
         )
     )
+    factor = -step_rate[0]
+
+    def step(mine, rest):
+        return (factor * (mine + rest.astype(F32))).astype(BF16)
+
+    sums, step_gate, step_up, step_down = lax.optimization_barrier(
+        (
+            sums,
+            step(in_own[:own], steps_rest[:own]),
+            step(in_own[own:], steps_rest[own:wide]),
+            step(out_own_steps, steps_rest[wide:]),
+        )
+    )
     out_rows = (tokens.astype(F32) + sums[:, :features]).astype(BF16)
     grad_in = (cotangent.astype(F32) + sums[:, features:]).astype(BF16)
-
-    acts_pair = move(acts, True, 0)
-    rows_rest = move(rows_pair, True, 0)
-    factor = -step_rate[0]
-    steps_in = dot(acts[:, :wide], rows_own[:, :features], TN) + dot(
-        acts_pair[:, :wide], rows_rest[:, :features], TN
-    )
-    steps_out = dot(acts[:, wide:], rows_own[:, features:], TN) + dot(
-        acts_pair[:, wide:], rows_rest[:, features:], TN
-    )
-    steps_in = (factor * steps_in).astype(BF16)
-    step_down = (factor * steps_out).astype(BF16)
-    return (out_rows, grad_in, steps_in[:own].T, steps_in[own:].T, step_down)
+    return (out_rows, grad_in, step_gate.T, step_up.T, step_down)
 
 
 def solution(mesh):

time: 227 us -> 226 us (level)
  blocking collectives: 164 us -> 146 us
  matrix products: 17.7 us -> 6.63 us
  waiting for transfers between devices: 8.16 us -> 19 us
  starting transfers between devices: 24.4 us -> 32.1 us
  local copies, waits for them, and re-layouts: 5.71 us -> 10.3 us
  other arithmetic: 3.76 us -> 7.12 us
    all_to_all x1 -> x0, blocking collectives: 18.8 us -> none  [layer(): lax.all_to_all(parts.reshape(members, count // members, tall), 'row', 0,...]
    all_to_all x0 -> x1, waiting for transfers between devices: none -> 11.4 us  [layer(): lax.all_to_all(parts.reshape(members, count // members, tall), 'row', 0,...]
    dot_general x12, matrix products: 17.7 us -> 6.63 us  [dot(): return lax.dot_general(left, right, dims, preferred_element_type=F32)]
    all_to_all x0 -> x1, starting transfers between devices: none -> 4.58 us  [layer(): lax.all_to_all(parts.reshape(members, count // members, tall), 'row', 0,...]
    ppermute x9 -> x8, starting transfers between devices: 20.2 us -> 23.2 us  [move(): return lax.ppermute(value, ('row', 'col'), pairs)]
    convert_element_type x0 -> x1, other arithmetic: none -> 2.67 us  [step(): return (factor * (mine + rest.astype(F32))).astype(BF16)]
    unnamed x24 -> x31, local copies, waits for them, and re-layouts: 3.27 us -> 5.91 us
    ppermute x9 -> x8, waiting for transfers between devices: 8.16 us -> 7.58 us  [move(): return lax.ppermute(value, ('row', 'col'), pairs)]
  transfers between devices with their start and end apart: 10 -> 10, of which waited for: 3 -> 4; matrix products, arithmetic and copies ran while one was open for 26% -> 28% of each run, Pallas kernels for 0% -> 0%
where the time goes in v4:
time: 226 us; the launch traced here: 224 us
  blocking collectives  146 us (65%)
  starting transfers between devices  32.1 us (14%)
  waiting for transfers between devices  19 us (8%)
  local copies, waits for them, and re-layouts  10.3 us (5%)
  other arithmetic  7.12 us (3%)
  matrix products  6.63 us (3%)
  between operations  2.37 us (1%)
    all_gather x1, blocking collectives, gather_col(): lax.all_gather(block, 'col', axis=0, tiled=True, axis_index_groups=every_...  79.2 us
    unnamed x1, blocking collectives  52.1 us
    ppermute x8, starting transfers between devices, move(): return lax.ppermute(value, ('row', 'col'), pairs)  23.2 us
    all_gather x1, blocking collectives, layer(): lax.all_gather(jnp.concatenate([back_gate, back_up, hidden], axis=1), 'ro...  14.8 us
    all_to_all x1, waiting for transfers between devices, layer(): lax.all_to_all(parts.reshape(members, count // members, tall), 'row', 0,...  11.4 us
    ppermute x8, waiting for transfers between devices, move(): return lax.ppermute(value, ('row', 'col'), pairs)  7.58 us
    dot_general x12, matrix products, dot(): return lax.dot_general(left, right, dims, preferred_element_type=F32)  6.63 us
    unnamed x31, local copies, waits for them, and re-layouts  5.91 us
  transfers between devices with their start and end apart: 10, of which 4 were waited for; matrix products, arithmetic and copies ran while one was open for 28% of the time, Pallas kernels for 0%

profile of v4, /device:TPU:40, one launch (start us, length us, event | category | flops | bytes accessed | tf_op | source)
XLA Modules:
  0.0 223.5 jit_solution(10203275839257485084)
XLA Ops:
  0.7 0.8 maximum_bitcast_fusion
  1.4 79.2 %all-gather = bf16[16,20,1024]{2,1,0:T(8,128)(2,1)S(1)} all-gather(bf16[1,20,1024]{2,1,0:T(8,128)(2,1)S(1)} %maximum_bitcast_fusion), channel_id=1, replica_groups={{0,2,4,6,8,10,12,14,16,18,20,22,24,26,28,30},{1,3,5,7,9,11,13,15,17,19,..., dimensions={0}, use_global_device_ids=true | all-gather | bytes 696320 | tf_op jit(solution)/shard_map/all_gather | solution.py:44
  80.6 0.1 reshape.24
  80.7 0.1 constant_dynamic-slice_fusion.1
  80.8 0.8 copy-done.1
  81.6 0.1 copy-done.4
  81.7 0.1 copy-done.5
  81.9 0.1 pad_maximum_fusion
  82.0 2.0 collective-permute-start.3
  83.9 2.4 %collective-permute-start.1 = (bf16[160,1024]{1,0:T(8,128)(2,1)S(1)}, bf16[160,1024]{1,0:T(8,128)(2,1)S(1)}, u32[]{:S(2)}, u32[]{:S(2)}) collective-permute-start(bf16[160,1024]{1,0:T(8,128)(2,1)S(1)} %get-tuple-element.23), channel_id=1, source_target_pairs={{0,32},{1,33},{2,34},{3,35},{4,36},{5,37},{6,38},{7,39},{8,40},{9,... | collective-permute-start | bytes 983048 | tf_op jit(solution)/shard_map/ppermute | solution.py:40
  86.4 3.6 %collective-permute-start.2 = (bf16[160,1024]{1,0:T(8,128)(2,1)S(1)}, bf16[160,1024]{1,0:T(8,128)(2,1)S(1)}, u32[]{:S(2)}, u32[]{:S(2)}) collective-permute-start(bf16[160,1024]{1,0:T(8,128)(2,1)S(1)} %get-tuple-element.23), channel_id=1, source_target_pairs={{0,63},{1,32},{2,33},{3,34},{4,35},{5,36},{6,37},{7,38},{8,39},{9,... | collective-permute-start | bytes 983048 | tf_op jit(solution)/shard_map/ppermute | solution.py:40
  90.0 4.1 %collective-permute-start = (bf16[160,1024]{1,0:T(8,128)(2,1)S(1)}, bf16[160,1024]{1,0:T(8,128)(2,1)S(1)}, u32[]{:S(2)}, u32[]{:S(2)}) collective-permute-start(bf16[160,1024]{1,0:T(8,128)(2,1)S(1)} %get-tuple-element.20), channel_id=1, source_target_pairs={{0,1},{1,2},{2,3},{3,4},{4,5},{5,6},{6,7},{7,8},{8,9},{9,10},{10,1... | collective-permute-start | bytes 983048 | tf_op jit(solution)/shard_map/ppermute | solution.py:40
  94.1 0.0 collective-permute-done.1
  94.2 1.8 collective-permute-done.2
  96.0 4.2 %collective-permute-done = bf16[160,1024]{1,0:T(8,128)(2,1)S(1)} collective-permute-done((bf16[160,1024]{1,0:T(8,128)(2,1)S(1)}, bf16[160,1024]{1,0:T(8,128)(2,1)S(1)}, u32[]{:S(2)}, u32[]{:S(2)}) %collective-permute-start) | collective-permute-done | bytes 327712 | tf_op jit(solution)/shard_map/ppermute | solution.py:40
  100.2 0.0 collective-permute-done.3
  100.3 0.4 fusion.20
  100.6 0.4 fusion.2
  101.0 0.4 copy-done.8
  101.4 0.5 fusion.5
  101.9 0.5 fusion.1
  102.5 1.0 pad_maximum_fusion.4
  103.5 4.6 %all-to-all-start = ((bf16[4,80,1344]{2,1,0:T(8,128)(2,1)}), bf16[4,80,1344]{2,1,0:T(8,128)(2,1)S(1)}, u32[]{:S(2)}, u32[]{:S(2)}) async-start(bf16[4,80,1344]{2,1,0:T(8,128)(2,1)} %bitcast.3), calls=%async_computation | async-start | bytes 1802240 | tf_op jit(solution)/shard_map/all_to_all | solution.py:88
  108.7 1.3 dynamic-slice.4
  110.6 11.4 %all-to-all-done = bf16[4,80,1344]{2,1,0:T(8,128)(2,1)S(1)} async-done(((bf16[4,80,1344]{2,1,0:T(8,128)(2,1)}), bf16[4,80,1344]{2,1,0:T(8,128)(2,1)S(1)}, u32[]{:S(2)}, u32[]{:S(2)}) %all-to-all-start) | async-done | bytes 860192 | tf_op jit(solution)/shard_map/all_to_all | solution.py:88
  122.0 0.1 convert_reduce_fusion
  122.2 0.1 multiply_convert_fusion.3
  122.3 0.1 concatenate.39
  122.4 14.8 %all_gather.7 = bf16[320,1344]{1,0:T(8,128)(2,1)S(1)} all-gather(bf16[80,1344]{1,0:T(8,128)(2,1)S(1)} %concatenate.39), channel_id=1, replica_groups={{0,64,128,192},{32,96,160,224},{1,65,129,193},{33,97,161,225},{2,66,130..., dimensions={0}, use_global_device_ids=true | all-gather | bytes 1075200 | tf_op jit(solution)/shard_map/all_gather | solution.py:103
  137.2 0.5 fusion.12
  137.7 0.3 fusion.23
  138.0 1.0 copy-done.9
  139.0 0.5 fusion.3
  139.5 0.3 fusion.18
  139.9 0.1 maximum_convert_fusion
  140.0 0.0 copy-start.7
  140.0 0.1 fusion.39
  140.1 1.0 copy-done.7
  141.1 0.4 convolution_convert_fusion.1
  141.5 0.7 convolution_convert_fusion
  142.2 2.0 collective-permute-start.6
  144.2 3.7 %collective-permute-start.5 = (bf16[160,1024]{1,0:T(8,128)(2,1)S(1)}, bf16[160,1024]{1,0:T(8,128)(2,1)S(1)}, u32[]{:S(2)}, u32[]{:S(2)}) collective-permute-start(bf16[160,1024]{1,0:T(8,128)(2,1)S(1)} %get-tuple-element.26), channel_id=1, source_target_pairs={{0,32},{1,33},{2,34},{3,35},{4,36},{5,37},{6,38},{7,39},{8,40},{9,... | collective-permute-start | bytes 983048 | tf_op jit(solution)/shard_map/ppermute | solution.py:40
  147.8 3.5 %collective-permute-start.4 = (bf16[160,1024]{1,0:T(8,128)(2,1)S(1)}, bf16[160,1024]{1,0:T(8,128)(2,1)S(1)}, u32[]{:S(2)}, u32[]{:S(2)}) collective-permute-start(bf16[160,1024]{1,0:T(8,128)(2,1)S(1)} %get-tuple-element.25), channel_id=1, source_target_pairs={{0,31},{1,0},{2,1},{3,2},{4,3},{5,4},{6,5},{7,6},{8,7},{9,8},{10,9... | collective-permute-start | bytes 983048 | tf_op jit(solution)/shard_map/ppermute | solution.py:40
  151.4 1.2 pad_maximum_fusion.1
  152.6 1.9 collective-permute-start.7
  154.5 0.7 fusion.16
  155.2 0.0 collective-permute-done.6
  155.2 0.0 collective-permute-done.5
  155.2 1.6 collective-permute-done.4
  156.8 0.2 fusion.11
  157.0 0.1 pad_maximum_fusion.2
  157.2 1.3 reshape.21
  158.5 1.5 pad.4
  160.0 1.3 reshape.22
  161.4 52.1 %fusion = f32[24,1024]{1,0:T(8,128)S(1)} fusion(f32[368,1024]{1,0:T(8,128)} %reshape.22), kind=kCustom, calls=%all-reduce-scatter | all-reduce-scatter fusion | flops 393217 | bytes 1607680
  213.5 4.3 %collective-permute-start.8 = (f32[15,1024]{1,0:T(8,128)S(1)}, f32[15,1024]{1,0:T(8,128)}, u32[]{:S(2)}, u32[]{:S(2)}) collective-permute-start(f32[15,1024]{1,0:T(8,128)S(1)} %slice.133), channel_id=1, source_target_pairs={{0,2},{2,4},{4,6},{6,8},{8,10},{10,12},{12,14},{14,16},{16,18},{18... | collective-permute-start | bytes 184328
  217.7 1.4 fusion.27
  219.2 0.0 collective-permute-done.8
  219.2 1.0 concatenate.44
  220.2 0.0 collective-permute-done.7
  220.2 0.0 copy-start.10
  220.2 0.0 copy-start.11
  220.2 2.7 %multiply_convert_fusion.1 = (bf16[448,512]{1,0:T(8,128)(2,1)}, bf16[448,512]{1,0:T(8,128)(2,1)}, bf16[448,512]{1,0:T(8,128)(2,1)}) fusion(f32[896,512]{1,0:T(8,128)S(1)} %fusion.16, bf16[1344,512]{1,0:T(8,128)(2,1)} %collective-permute-done.7, f32[]{:T(128)} %bitcast.4, f32[448,512]{1,0:T(8,128)S(1)} %fusion.27), kind=kLoop, calls=%fused_computation.15 | loop fusion | flops 2752512 | bytes 5505028 | tf_op jit(solution)/shard_map/convert_element_type | solution.py:147
  222.9 0.6 add_convert_fusion
  (21 shorter events, 0.1 us)
Async XLA Ops:
  80.6 1.0 copy-start.1
  80.6 1.2 copy-start.4
  80.6 1.3 copy-start.5
  82.0 18.3 %collective-permute-start.3 = (bf16[1344,512]{1,0:T(8,128)(2,1)S(1)}, bf16[1344,512]{1,0:T(8,128)(2,1)S(1)}, u32[]{:S(2)}, u32[]{:S(2)}) collective-permute-start(bf16[1344,512]{1,0:T(8,128)(2,1)S(1)} %pad_maximum_fusion), channel_id=1, source_target_pairs={{0,32},{1,33},{2,34},{3,35},{4,36},{5,37},{6,38},{7,39},{8,40},{9,... | collective-permute-start | bytes 4128776 | tf_op jit(solution)/shard_map/ppermute | solution.py:40
  83.9 10.2 %collective-permute-start.1 = (bf16[160,1024]{1,0:T(8,128)(2,1)S(1)}, bf16[160,1024]{1,0:T(8,128)(2,1)S(1)}, u32[]{:S(2)}, u32[]{:S(2)}) collective-permute-start(bf16[160,1024]{1,0:T(8,128)(2,1)S(1)} %get-tuple-element.23), channel_id=1, source_target_pairs={{0,32},{1,33},{2,34},{3,35},{4,36},{5,37},{6,38},{7,39},{8,40},{9,... | collective-permute-start | bytes 983048 | tf_op jit(solution)/shard_map/ppermute | solution.py:40
  86.4 9.6 %collective-permute-start.2 = (bf16[160,1024]{1,0:T(8,128)(2,1)S(1)}, bf16[160,1024]{1,0:T(8,128)(2,1)S(1)}, u32[]{:S(2)}, u32[]{:S(2)}) collective-permute-start(bf16[160,1024]{1,0:T(8,128)(2,1)S(1)} %get-tuple-element.23), channel_id=1, source_target_pairs={{0,63},{1,32},{2,33},{3,34},{4,35},{5,36},{6,37},{7,38},{8,39},{9,... | collective-permute-start | bytes 983048 | tf_op jit(solution)/shard_map/ppermute | solution.py:40
  90.0 10.2 %collective-permute-start = (bf16[160,1024]{1,0:T(8,128)(2,1)S(1)}, bf16[160,1024]{1,0:T(8,128)(2,1)S(1)}, u32[]{:S(2)}, u32[]{:S(2)}) collective-permute-start(bf16[160,1024]{1,0:T(8,128)(2,1)S(1)} %get-tuple-element.20), channel_id=1, source_target_pairs={{0,1},{1,2},{2,3},{3,4},{4,5},{5,6},{6,7},{7,8},{8,9},{9,10},{10,1... | collective-permute-start | bytes 983048 | tf_op jit(solution)/shard_map/ppermute | solution.py:40
  96.0 5.0 %copy-start.6 = (bf16[320,1024]{1,0:T(8,128)(2,1)}, bf16[320,1024]{1,0:T(8,128)(2,1)S(1)}, u32[]{:S(2)}) copy-start(bf16[320,1024]{1,0:T(8,128)(2,1)S(1)} %constant_dynamic-update-slice_fusion.2) | copy-start | bytes 1966084
  100.2 54.3 %copy-start.2 = (bf16[320,1024]{1,0:T(8,128)(2,1)}, bf16[320,1024]{1,0:T(8,128)(2,1)S(1)}, u32[]{:S(2)}) copy-start(bf16[320,1024]{1,0:T(8,128)(2,1)S(1)} %constant_dynamic-update-slice_fusion) | copy-start | bytes 1966084
  100.3 1.1 copy-start.8
  103.5 18.6 %all-to-all-start = ((bf16[4,80,1344]{2,1,0:T(8,128)(2,1)}), bf16[4,80,1344]{2,1,0:T(8,128)(2,1)S(1)}, u32[]{:S(2)}, u32[]{:S(2)}) async-start(bf16[4,80,1344]{2,1,0:T(8,128)(2,1)} %bitcast.3), calls=%async_computation | async-start | bytes 1802240 | tf_op jit(solution)/shard_map/all_to_all | solution.py:88
  137.2 17.3 %copy-start = (bf16[320,1344]{1,0:T(8,128)(2,1)}, bf16[320,1344]{1,0:T(8,128)(2,1)S(1)}, u32[]{:S(2)}) copy-start(bf16[320,1344]{1,0:T(8,128)(2,1)S(1)} %all_gather.7) | copy-start | bytes 2580484
  137.7 1.3 copy-start.9
  140.0 1.1 copy-start.7
  142.2 13.0 %collective-permute-start.6 = (bf16[160,1024]{1,0:T(8,128)(2,1)S(1)}, bf16[160,1024]{1,0:T(8,128)(2,1)S(1)}, u32[]{:S(2)}, u32[]{:S(2)}) collective-permute-start(bf16[160,1024]{1,0:T(8,128)(2,1)S(1)} %get-tuple-element.27), channel_id=1, source_target_pairs={{0,63},{1,32},{2,33},{3,34},{4,35},{5,36},{6,37},{7,38},{8,39},{9,... | collective-permute-start | bytes 983048 | tf_op jit(solution)/shard_map/ppermute | solution.py:40
  144.2 11.1 %collective-permute-start.5 = (bf16[160,1024]{1,0:T(8,128)(2,1)S(1)}, bf16[160,1024]{1,0:T(8,128)(2,1)S(1)}, u32[]{:S(2)}, u32[]{:S(2)}) collective-permute-start(bf16[160,1024]{1,0:T(8,128)(2,1)S(1)} %get-tuple-element.26), channel_id=1, source_target_pairs={{0,32},{1,33},{2,34},{3,35},{4,36},{5,37},{6,38},{7,39},{8,40},{9,... | collective-permute-start | bytes 983048 | tf_op jit(solution)/shard_map/ppermute | solution.py:40
  147.8 9.0 %collective-permute-start.4 = (bf16[160,1024]{1,0:T(8,128)(2,1)S(1)}, bf16[160,1024]{1,0:T(8,128)(2,1)S(1)}, u32[]{:S(2)}, u32[]{:S(2)}) collective-permute-start(bf16[160,1024]{1,0:T(8,128)(2,1)S(1)} %get-tuple-element.25), channel_id=1, source_target_pairs={{0,31},{1,0},{2,1},{3,2},{4,3},{5,4},{6,5},{7,6},{8,7},{9,8},{10,9... | collective-permute-start | bytes 983048 | tf_op jit(solution)/shard_map/ppermute | solution.py:40
  152.6 67.6 %collective-permute-start.7 = (bf16[1344,512]{1,0:T(8,128)(2,1)}, bf16[1344,512]{1,0:T(8,128)(2,1)}, u32[]{:S(2)}, u32[]{:S(2)}) collective-permute-start(bf16[1344,512]{1,0:T(8,128)(2,1)} %pad_maximum_fusion.1), channel_id=1, source_target_pairs={{0,32},{1,33},{2,34},{3,35},{4,36},{5,37},{6,38},{7,39},{8,40},{9,... | collective-permute-start | bytes 4128776 | tf_op jit(solution)/shard_map/ppermute | solution.py:40
  161.4 56.4 %copy-start.3 = (bf16[320,1024]{1,0:T(8,128)(2,1)S(1)}, bf16[320,1024]{1,0:T(8,128)(2,1)}, u32[]{:S(2)}) copy-start(bf16[320,1024]{1,0:T(8,128)(2,1)} %copy-done.2) | copy-start | bytes 1966084
  213.5 5.7 %collective-permute-start.8 = (f32[15,1024]{1,0:T(8,128)S(1)}, f32[15,1024]{1,0:T(8,128)}, u32[]{:S(2)}, u32[]{:S(2)}) collective-permute-start(f32[15,1024]{1,0:T(8,128)S(1)} %slice.133), channel_id=1, source_target_pairs={{0,2},{2,4},{4,6},{6,8},{8,10},{10,12},{12,14},{14,16},{16,18},{18... | collective-permute-start | bytes 184328
  220.2 2.7 %copy-start.10 = (bf16[20,512]{1,0:T(8,128)(2,1)S(1)}, bf16[20,512]{1,0:T(8,128)(2,1)}, u32[]{:S(2)}) copy-start(bf16[20,512]{1,0:T(8,128)(2,1)} %param.10) | copy-start | bytes 61444
  220.2 2.7 %copy-start.11 = (bf16[20,512]{1,0:T(8,128)(2,1)S(1)}, bf16[20,512]{1,0:T(8,128)(2,1)}, u32[]{:S(2)}) copy-start(bf16[20,512]{1,0:T(8,128)(2,1)} %param.6) | copy-start | bytes 61444

commit v5 on v4

--- a/solution.py
+++ b/solution.py
@@ -1,7 +1,9 @@
 import jax
 import jax.numpy as jnp
 from jax import lax
+from jax.experimental import pallas as pl
 from jax.experimental.layout import Layout, with_layout_constraint
+from jax.experimental.pallas import tpu as pltpu
 from jax.sharding import PartitionSpec as P
 
 
@@ -44,13 +46,50 @@
     return lax.all_gather(block, "col", axis=0, tiled=True, axis_index_groups=every_other("col"))
 
 
-def scatter_col(parts):
-    members = lax.axis_size("col") // 2
-    rows = parts.shape[0] // members
-    width = parts.shape[1]
-    padded = round_up(rows + 1, 8) - 1
-    parts = parts.reshape(members, rows, width)
-    parts = jnp.pad(parts, ((0, 0), (0, padded - rows), (0, 0))).reshape(members * padded, width)
+def spread(core, out_own, grad_own, near, pair, far, rows, padded):
+    half, width = near.shape
+    features = out_own.shape[1]
+    blocks = half // rows
+
+    def kernel(core_ref, out_ref, grad_ref, near_ref, pair_ref, far_ref, sums_ref, same_ref, cross_ref):
+        near_rows = near_ref[...].astype(F32)
+        same_ref[:, :features] = out_ref[...] + near_rows[:, :features]
+        same_ref[:, features:] = grad_ref[...] + near_rows[:, features:]
+        cross_ref[...] = pair_ref[...].astype(F32) + far_ref[...].astype(F32)
+        for block in range(2 * blocks):
+            gap = padded - rows
+            sums_ref[block * padded + rows : (block + 1) * padded, :] = jnp.zeros((gap, width), F32)
+
+        def write(low, high):
+            for block in range(blocks):
+                source = slice(block * rows, (block + 1) * rows)
+                for offset, part in ((0, low), (blocks, high)):
+                    start = (offset + block) * padded
+                    sums_ref[start : start + rows, :] = part[source, :]
+
+        @pl.when(core_ref[0] == 0)
+        def _():
+            write(same_ref, cross_ref)
+
+        @pl.when(core_ref[0] != 0)
+        def _():
+            write(cross_ref, same_ref)
+
+    whole = pl.BlockSpec((half, width), lambda _: (0, 0))
+    upper = pl.BlockSpec((half, features), lambda _: (0, 0))
+    return pl.pallas_call(
+        kernel,
+        grid=(1,),
+        out_shape=jax.ShapeDtypeStruct((2 * blocks * padded, width), F32),
+        in_specs=[pl.BlockSpec(memory_space=pltpu.SMEM), upper, upper, whole, whole, whole],
+        out_specs=pl.BlockSpec((2 * blocks * padded, width), lambda _: (0, 0)),
+        scratch_shapes=[pltpu.VMEM((half, width), F32), pltpu.VMEM((half, width), F32)],
+        compiler_params=pltpu.CompilerParams(vmem_limit_bytes=16 << 20),
+        name="spread",
+    )(core[None], out_own, grad_own, near, pair, far)
+
+
+def scatter_col(parts, rows):
     summed = lax.psum_scatter(
         parts, "col", scatter_dimension=0, tiled=True, axis_index_groups=every_other("col")
     )
@@ -61,7 +100,6 @@
     features = tokens.shape[1]
     own = w_gate.shape[1]
     core = lax.axis_index("row") % 2
-    first = core == 0
     gathered = gather_col(jnp.concatenate([tokens, cotangent], axis=1))
     count = gathered.shape[0]
     half = count // 2
@@ -109,20 +147,18 @@
     )
 
     def outputs(matrix):
-        return row_major(
-            jnp.concatenate(
-                [dot(acts[:, wide:], matrix[wide:], NN), dot(acts[:, :wide], matrix[:wide], NN)],
-                axis=1,
-            )
-        )
-
-    out_pair = outputs(weights_pair).astype(BF16)
-    out_own = outputs(weights)
-    far, near, pair = out_pair[half:], out_own[half:].astype(BF16), out_pair[:half]
-    far, near, pair, held = lax.optimization_barrier((far, near, pair, acts))
+        return [
+            row_major(dot(acts[:, wide:], matrix[wide:], NN)),
+            row_major(dot(acts[:, :wide], matrix[:wide], NN)),
+        ]
+
+    out_pair = jnp.concatenate([value.astype(BF16) for value in outputs(weights_pair)], axis=1)
+    out_own, grad_own = outputs(weights)
+    near = jnp.concatenate([out_own[half:].astype(BF16), grad_own[half:].astype(BF16)], axis=1)
+    pair, far, near, held = lax.optimization_barrier((out_pair[:half], out_pair[half:], near, acts))
+    pair = move(pair, True, 0)
     far = move(far, True, -1)
     near = move(near, False, -1)
-    pair = move(pair, True, 0)
 
     def partial_steps(rows):
         return [
@@ -132,15 +168,12 @@
 
     steps_rest = [value.astype(BF16) for value in partial_steps(rows_pair)]
     steps_rest = move(jnp.concatenate(steps_rest, axis=0), True, 0)
-    in_own, out_own_steps = lax.optimization_barrier(partial_steps(rows_own))
-
-    sum_same = out_own[:half] + near.astype(F32)
-    sum_cross = pair.astype(F32) + far.astype(F32)
-    sums = scatter_col(
-        jnp.concatenate(
-            [jnp.where(first, sum_same, sum_cross), jnp.where(first, sum_cross, sum_same)], axis=0
-        )
-    )
+    in_own, last_own = partial_steps(rows_own)
+    in_own, last_own = lax.optimization_barrier((in_own, last_own))
+
+    rows = tokens.shape[0]
+    padded = round_up(rows + 1, 8) - 1
+    sums = scatter_col(spread(core, out_own, grad_own, near, pair, far, rows, padded), rows)
     factor = -step_rate[0]
 
     def step(mine, rest):
@@ -151,7 +184,7 @@
             sums,
             step(in_own[:own], steps_rest[:own]),
             step(in_own[own:], steps_rest[own:wide]),
-            step(out_own_steps, steps_rest[wide:]),
+            step(last_own, steps_rest[wide:]),
         )
     )
     out_rows = (tokens.astype(F32) + sums[:, :features]).astype(BF16)

time: 226 us -> 218 us (0.965)
  local copies, waits for them, and re-layouts: 10.3 us -> 4.76 us
    reshape x2 -> x0, local copies, waits for them, and re-layouts: 2.65 us -> none  [the longest x1 1.35 us: scatter_col(): jnp.pad(parts, ((0, 0), (0, padded - rows), (0, 0)))]
    unnamed x31 -> x29, local copies, waits for them, and re-layouts: 5.91 us -> 4.5 us
  transfers between devices with their start and end apart: 10 -> 10, of which waited for: 4 -> 5; matrix products, arithmetic and copies ran while one was open for 28% -> 26% of each run, Pallas kernels for 0% -> 0%
where the time goes in v5:
time: 218 us; the launch traced here: 217 us
  blocking collectives  145 us (67%)
  starting transfers between devices  30.9 us (14%)
  waiting for transfers between devices  20.4 us (9%)
  other arithmetic  6.72 us (3%)
  matrix products  6.72 us (3%)
  local copies, waits for them, and re-layouts  4.76 us (2%)
  between operations  2.36 us (1%)
    all_gather x1, blocking collectives, gather_col(): lax.all_gather(block, 'col', axis=0, tiled=True, axis_index_groups=every_...  79.2 us
    unnamed x1, blocking collectives  51.3 us
    ppermute x8, starting transfers between devices, move(): return lax.ppermute(value, ('row', 'col'), pairs)  22 us
    all_gather x1, blocking collectives, layer(): lax.all_gather(jnp.concatenate([back_gate, back_up, hidden], axis=1), 'ro...  14.8 us
    all_to_all x1, waiting for transfers between devices, layer(): lax.all_to_all(parts.reshape(members, count // members, tall), 'row', 0,...  11.4 us
    ppermute x8, waiting for transfers between devices, move(): return lax.ppermute(value, ('row', 'col'), pairs)  8.55 us
    dot_general x12, matrix products, dot(): return lax.dot_general(left, right, dims, preferred_element_type=F32)  6.72 us
    all_to_all x1, starting transfers between devices, layer(): lax.all_to_all(parts.reshape(members, count // members, tall), 'row', 0,...  4.58 us
  transfers between devices with their start and end apart: 10, of which 5 were waited for; matrix products, arithmetic and copies ran while one was open for 26% of the time, Pallas kernels for 0%

profile of v5, /device:TPU:40, one launch (start us, length us, event | category | flops | bytes accessed | tf_op | source)
XLA Modules:
  0.0 217.3 jit_solution(5054103871996932560)
XLA Ops:
  0.7 0.8 maximum_bitcast_fusion
  1.4 79.2 %all-gather = bf16[16,20,1024]{2,1,0:T(8,128)(2,1)S(1)} all-gather(bf16[1,20,1024]{2,1,0:T(8,128)(2,1)S(1)} %maximum_bitcast_fusion), channel_id=1, replica_groups={{0,2,4,6,8,10,12,14,16,18,20,22,24,26,28,30},{1,3,5,7,9,11,13,15,17,19,..., dimensions={0}, use_global_device_ids=true | all-gather | bytes 696320 | tf_op jit(solution)/shard_map/all_gather | solution.py:46
  80.6 0.1 reshape.16
  80.7 0.1 constant_dynamic-slice_fusion.1
  80.8 0.8 copy-done.1
  81.6 0.1 copy-done.3
  81.7 0.1 copy-done.4
  81.9 0.1 pad_maximum_fusion
  82.0 2.0 collective-permute-start.3
  83.9 2.4 %collective-permute-start.1 = (bf16[160,1024]{1,0:T(8,128)(2,1)S(1)}, bf16[160,1024]{1,0:T(8,128)(2,1)S(1)}, u32[]{:S(2)}, u32[]{:S(2)}) collective-permute-start(bf16[160,1024]{1,0:T(8,128)(2,1)S(1)} %get-tuple-element.23), channel_id=1, source_target_pairs={{0,32},{1,33},{2,34},{3,35},{4,36},{5,37},{6,38},{7,39},{8,40},{9,... | collective-permute-start | bytes 983048 | tf_op jit(solution)/shard_map/ppermute | solution.py:42
  86.4 3.6 %collective-permute-start.2 = (bf16[160,1024]{1,0:T(8,128)(2,1)S(1)}, bf16[160,1024]{1,0:T(8,128)(2,1)S(1)}, u32[]{:S(2)}, u32[]{:S(2)}) collective-permute-start(bf16[160,1024]{1,0:T(8,128)(2,1)S(1)} %get-tuple-element.23), channel_id=1, source_target_pairs={{0,63},{1,32},{2,33},{3,34},{4,35},{5,36},{6,37},{7,38},{8,39},{9,... | collective-permute-start | bytes 983048 | tf_op jit(solution)/shard_map/ppermute | solution.py:42
  90.0 4.1 %collective-permute-start = (bf16[160,1024]{1,0:T(8,128)(2,1)S(1)}, bf16[160,1024]{1,0:T(8,128)(2,1)S(1)}, u32[]{:S(2)}, u32[]{:S(2)}) collective-permute-start(bf16[160,1024]{1,0:T(8,128)(2,1)S(1)} %get-tuple-element.20), channel_id=1, source_target_pairs={{0,1},{1,2},{2,3},{3,4},{4,5},{5,6},{6,7},{7,8},{8,9},{9,10},{10,1... | collective-permute-start | bytes 983048 | tf_op jit(solution)/shard_map/ppermute | solution.py:42
  94.1 0.0 collective-permute-done.1
  94.2 1.8 collective-permute-done.2
  96.0 0.0 copy-start.5
  96.0 4.2 %collective-permute-done = bf16[160,1024]{1,0:T(8,128)(2,1)S(1)} collective-permute-done((bf16[160,1024]{1,0:T(8,128)(2,1)S(1)}, bf16[160,1024]{1,0:T(8,128)(2,1)S(1)}, u32[]{:S(2)}, u32[]{:S(2)}) %collective-permute-start) | collective-permute-done | bytes 327712 | tf_op jit(solution)/shard_map/ppermute | solution.py:42
  100.2 0.0 copy-start.2
  100.2 0.0 collective-permute-done.3
  100.3 0.0 copy-start.7
  100.3 0.4 fusion.13
  100.6 0.4 fusion.2
  101.0 0.0 copy-done.5
  101.0 0.4 copy-done.7
  101.4 0.5 fusion.4
  101.9 0.5 fusion.1
  102.5 1.0 pad_maximum_fusion.3
  103.5 4.6 %all-to-all-start = ((bf16[4,80,1344]{2,1,0:T(8,128)(2,1)}), bf16[4,80,1344]{2,1,0:T(8,128)(2,1)S(1)}, u32[]{:S(2)}, u32[]{:S(2)}) async-start(bf16[4,80,1344]{2,1,0:T(8,128)(2,1)} %bitcast.4), calls=%async_computation | async-start | bytes 1802240 | tf_op jit(solution)/shard_map/all_to_all | solution.py:126
  108.7 1.3 dynamic-slice.4
  110.6 11.4 %all-to-all-done = bf16[4,80,1344]{2,1,0:T(8,128)(2,1)S(1)} async-done(((bf16[4,80,1344]{2,1,0:T(8,128)(2,1)}), bf16[4,80,1344]{2,1,0:T(8,128)(2,1)S(1)}, u32[]{:S(2)}, u32[]{:S(2)}) %all-to-all-start) | async-done | bytes 860192 | tf_op jit(solution)/shard_map/all_to_all | solution.py:126
  122.1 0.1 convert_reduce_fusion
  122.2 0.1 multiply_convert_fusion.3
  122.3 0.1 concatenate.36
  122.4 14.8 %all_gather.7 = bf16[320,1344]{1,0:T(8,128)(2,1)S(1)} all-gather(bf16[80,1344]{1,0:T(8,128)(2,1)S(1)} %concatenate.36), channel_id=1, replica_groups={{0,64,128,192},{32,96,160,224},{1,65,129,193},{33,97,161,225},{2,66,130..., dimensions={0}, use_global_device_ids=true | all-gather | bytes 1075200 | tf_op jit(solution)/shard_map/all_gather | solution.py:141
  137.2 0.3 fusion.17.out_ref
  137.5 0.0 copy-start.8
  137.5 0.5 fusion.6.grad_ref
  138.1 0.8 copy-done.8
  138.9 0.5 convolution_convert_fusion.2
  139.4 0.0 copy-start.6
  139.4 0.3 convolution_convert_fusion.3
  139.7 0.1 pad_maximum_fusion.6
  139.9 0.6 copy-done.6
  140.5 0.4 convolution_convert_fusion.1
  140.9 0.7 convolution_convert_fusion
  141.6 2.8 %collective-permute-start.4 = (bf16[160,1024]{1,0:T(8,128)(2,1)S(1)}, bf16[160,1024]{1,0:T(8,128)(2,1)S(1)}, u32[]{:S(2)}, u32[]{:S(2)}) collective-permute-start(bf16[160,1024]{1,0:T(8,128)(2,1)S(1)} %get-tuple-element.25), channel_id=1, source_target_pairs={{0,31},{1,0},{2,1},{3,2},{4,3},{5,4},{6,5},{7,6},{8,7},{9,8},{10,9... | collective-permute-start | bytes 983048 | tf_op jit(solution)/shard_map/ppermute | solution.py:42
  144.4 2.0 collective-permute-start.5
  146.4 2.1 collective-permute-start.6
  148.4 1.2 pad_maximum_fusion.1
  149.6 3.1 %collective-permute-start.7 = (bf16[1344,512]{1,0:T(8,128)(2,1)}, bf16[1344,512]{1,0:T(8,128)(2,1)}, u32[]{:S(2)}, u32[]{:S(2)}) collective-permute-start(bf16[1344,512]{1,0:T(8,128)(2,1)} %pad_maximum_fusion.1), channel_id=1, source_target_pairs={{0,32},{1,33},{2,34},{3,35},{4,36},{5,37},{6,38},{7,39},{8,40},{9,... | collective-permute-start | bytes 4128776 | tf_op jit(solution)/shard_map/ppermute | solution.py:42
  152.7 0.7 fusion.10
  153.4 0.0 collective-permute-done.4.near_ref
  153.4 0.0 collective-permute-done.5.pair_ref
  153.4 2.6 %collective-permute-done.6.far_ref = bf16[160,1024]{1,0:T(8,128)(2,1)S(1)} collective-permute-done((bf16[160,1024]{1,0:T(8,128)(2,1)S(1)}, bf16[160,1024]{1,0:T(8,128)(2,1)S(1)}, u32[]{:S(2)}, u32[]{:S(2)}) %collective-permute-start.6) | collective-permute-done | bytes 327712 | tf_op jit(solution)/shard_map/ppermute | solution.py:42
  156.0 0.3 spread.1
  156.3 51.3 %fusion = f32[24,1024]{1,0:T(8,128)S(1)} fusion(f32[368,1024]{1,0:T(8,128)S(1)} %spread.1), kind=kCustom, calls=%all-reduce-scatter | all-reduce-scatter fusion | flops 393217 | bytes 1607680
  207.7 4.3 %collective-permute-start.8 = (f32[15,1024]{1,0:T(8,128)S(1)}, f32[15,1024]{1,0:T(8,128)S(1)}, u32[]{:S(2)}, u32[]{:S(2)}) collective-permute-start(f32[15,1024]{1,0:T(8,128)S(1)} %slice.134), channel_id=1, source_target_pairs={{0,2},{2,4},{4,6},{6,8},{8,10},{10,12},{12,14},{14,16},{16,18},{18... | collective-permute-start | bytes 184328
  211.9 1.5 fusion.21
  213.4 0.4 collective-permute-done.8
  213.8 0.2 concatenate.40
  214.0 0.0 collective-permute-done.7
  214.0 0.0 copy-start.9
  214.0 0.0 copy-start.10
  214.0 2.7 %multiply_convert_fusion.1 = (bf16[448,512]{1,0:T(8,128)(2,1)}, bf16[448,512]{1,0:T(8,128)(2,1)}, bf16[448,512]{1,0:T(8,128)(2,1)}) fusion(f32[896,512]{1,0:T(8,128)S(1)} %fusion.10, bf16[1344,512]{1,0:T(8,128)(2,1)} %collective-permute-done.7, f32[]{:T(128)} %bitcast.5, f32[448,512]{1,0:T(8,128)S(1)} %fusion.21), kind=kLoop, calls=%fused_computation.13 | loop fusion | flops 2752512 | bytes 5505028 | tf_op jit(solution)/shard_map/convert_element_type | solution.py:180
  216.7 0.6 add_convert_fusion
  (16 shorter events, 0.2 us)
Async XLA Ops:
  80.6 1.0 copy-start.1
  80.6 1.2 copy-start.3
  80.6 1.3 copy-start.4
  82.0 18.3 %collective-permute-start.3 = (bf16[1344,512]{1,0:T(8,128)(2,1)S(1)}, bf16[1344,512]{1,0:T(8,128)(2,1)S(1)}, u32[]{:S(2)}, u32[]{:S(2)}) collective-permute-start(bf16[1344,512]{1,0:T(8,128)(2,1)S(1)} %pad_maximum_fusion), channel_id=1, source_target_pairs={{0,32},{1,33},{2,34},{3,35},{4,36},{5,37},{6,38},{7,39},{8,40},{9,... | collective-permute-start | bytes 4128776 | tf_op jit(solution)/shard_map/ppermute | solution.py:42
  83.9 10.2 %collective-permute-start.1 = (bf16[160,1024]{1,0:T(8,128)(2,1)S(1)}, bf16[160,1024]{1,0:T(8,128)(2,1)S(1)}, u32[]{:S(2)}, u32[]{:S(2)}) collective-permute-start(bf16[160,1024]{1,0:T(8,128)(2,1)S(1)} %get-tuple-element.23), channel_id=1, source_target_pairs={{0,32},{1,33},{2,34},{3,35},{4,36},{5,37},{6,38},{7,39},{8,40},{9,... | collective-permute-start | bytes 983048 | tf_op jit(solution)/shard_map/ppermute | solution.py:42
  86.4 9.6 %collective-permute-start.2 = (bf16[160,1024]{1,0:T(8,128)(2,1)S(1)}, bf16[160,1024]{1,0:T(8,128)(2,1)S(1)}, u32[]{:S(2)}, u32[]{:S(2)}) collective-permute-start(bf16[160,1024]{1,0:T(8,128)(2,1)S(1)} %get-tuple-element.23), channel_id=1, source_target_pairs={{0,63},{1,32},{2,33},{3,34},{4,35},{5,36},{6,37},{7,38},{8,39},{9,... | collective-permute-start | bytes 983048 | tf_op jit(solution)/shard_map/ppermute | solution.py:42
  90.0 10.2 %collective-permute-start = (bf16[160,1024]{1,0:T(8,128)(2,1)S(1)}, bf16[160,1024]{1,0:T(8,128)(2,1)S(1)}, u32[]{:S(2)}, u32[]{:S(2)}) collective-permute-start(bf16[160,1024]{1,0:T(8,128)(2,1)S(1)} %get-tuple-element.20), channel_id=1, source_target_pairs={{0,1},{1,2},{2,3},{3,4},{4,5},{5,6},{6,7},{7,8},{8,9},{9,10},{10,1... | collective-permute-start | bytes 983048 | tf_op jit(solution)/shard_map/ppermute | solution.py:42
  96.0 5.0 %copy-start.5 = (bf16[320,1024]{1,0:T(8,128)(2,1)}, bf16[320,1024]{1,0:T(8,128)(2,1)S(1)}, u32[]{:S(2)}) copy-start(bf16[320,1024]{1,0:T(8,128)(2,1)S(1)} %constant_dynamic-update-slice_fusion.2) | copy-start | bytes 1966084
  100.2 52.5 %copy-start.2 = (bf16[320,1024]{1,0:T(8,128)(2,1)}, bf16[320,1024]{1,0:T(8,128)(2,1)S(1)}, u32[]{:S(2)}) copy-start(bf16[320,1024]{1,0:T(8,128)(2,1)S(1)} %constant_dynamic-update-slice_fusion) | copy-start | bytes 1966084
  100.3 1.1 copy-start.7
  103.5 18.6 %all-to-all-start = ((bf16[4,80,1344]{2,1,0:T(8,128)(2,1)}), bf16[4,80,1344]{2,1,0:T(8,128)(2,1)S(1)}, u32[]{:S(2)}, u32[]{:S(2)}) async-start(bf16[4,80,1344]{2,1,0:T(8,128)(2,1)} %bitcast.4), calls=%async_computation | async-start | bytes 1802240 | tf_op jit(solution)/shard_map/all_to_all | solution.py:126
  137.2 15.5 %copy-start = (bf16[320,1344]{1,0:T(8,128)(2,1)}, bf16[320,1344]{1,0:T(8,128)(2,1)S(1)}, u32[]{:S(2)}) copy-start(bf16[320,1344]{1,0:T(8,128)(2,1)S(1)} %all_gather.7) | copy-start | bytes 2580484
  137.5 1.3 copy-start.8
  139.4 1.1 copy-start.6
  141.6 11.8 %collective-permute-start.4 = (bf16[160,1024]{1,0:T(8,128)(2,1)S(1)}, bf16[160,1024]{1,0:T(8,128)(2,1)S(1)}, u32[]{:S(2)}, u32[]{:S(2)}) collective-permute-start(bf16[160,1024]{1,0:T(8,128)(2,1)S(1)} %get-tuple-element.25), channel_id=1, source_target_pairs={{0,31},{1,0},{2,1},{3,2},{4,3},{5,4},{6,5},{7,6},{8,7},{9,8},{10,9... | collective-permute-start | bytes 983048 | tf_op jit(solution)/shard_map/ppermute | solution.py:42
  144.4 9.0 %collective-permute-start.5 = (bf16[160,1024]{1,0:T(8,128)(2,1)S(1)}, bf16[160,1024]{1,0:T(8,128)(2,1)S(1)}, u32[]{:S(2)}, u32[]{:S(2)}) collective-permute-start(bf16[160,1024]{1,0:T(8,128)(2,1)S(1)} %get-tuple-element.26), channel_id=1, source_target_pairs={{0,32},{1,33},{2,34},{3,35},{4,36},{5,37},{6,38},{7,39},{8,40},{9,... | collective-permute-start | bytes 983048 | tf_op jit(solution)/shard_map/ppermute | solution.py:42
  146.4 9.6 %collective-permute-start.6 = (bf16[160,1024]{1,0:T(8,128)(2,1)S(1)}, bf16[160,1024]{1,0:T(8,128)(2,1)S(1)}, u32[]{:S(2)}, u32[]{:S(2)}) collective-permute-start(bf16[160,1024]{1,0:T(8,128)(2,1)S(1)} %get-tuple-element.27), channel_id=1, source_target_pairs={{0,63},{1,32},{2,33},{3,34},{4,35},{5,36},{6,37},{7,38},{8,39},{9,... | collective-permute-start | bytes 983048 | tf_op jit(solution)/shard_map/ppermute | solution.py:42
  149.6 64.4 %collective-permute-start.7 = (bf16[1344,512]{1,0:T(8,128)(2,1)}, bf16[1344,512]{1,0:T(8,128)(2,1)}, u32[]{:S(2)}, u32[]{:S(2)}) collective-permute-start(bf16[1344,512]{1,0:T(8,128)(2,1)} %pad_maximum_fusion.1), channel_id=1, source_target_pairs={{0,32},{1,33},{2,34},{3,35},{4,36},{5,37},{6,38},{7,39},{8,40},{9,... | collective-permute-start | bytes 4128776 | tf_op jit(solution)/shard_map/ppermute | solution.py:42
  207.7 6.2 %collective-permute-start.8 = (f32[15,1024]{1,0:T(8,128)S(1)}, f32[15,1024]{1,0:T(8,128)S(1)}, u32[]{:S(2)}, u32[]{:S(2)}) collective-permute-start(f32[15,1024]{1,0:T(8,128)S(1)} %slice.134), channel_id=1, source_target_pairs={{0,2},{2,4},{4,6},{6,8},{8,10},{10,12},{12,14},{14,16},{16,18},{18... | collective-permute-start | bytes 184328
  214.0 2.7 %copy-start.9 = (bf16[20,512]{1,0:T(8,128)(2,1)S(1)}, bf16[20,512]{1,0:T(8,128)(2,1)}, u32[]{:S(2)}) copy-start(bf16[20,512]{1,0:T(8,128)(2,1)} %param.10) | copy-start | bytes 61444
  214.0 2.7 %copy-start.10 = (bf16[20,512]{1,0:T(8,128)(2,1)S(1)}, bf16[20,512]{1,0:T(8,128)(2,1)}, u32[]{:S(2)}) copy-start(bf16[20,512]{1,0:T(8,128)(2,1)} %param.6) | copy-start | bytes 61444

commit v6 on v5

--- a/solution.py
+++ b/solution.py
@@ -89,6 +89,64 @@
     )(core[None], out_own, grad_own, near, pair, far)
 
 
+def pick(order, wide_part, narrow_part):
+    count, wide = wide_part.shape
+    width = wide + narrow_part.shape[1]
+    chunk = count // order.shape[0]
+
+    def kernel(order_ref, wide_ref, narrow_ref, send_ref, keep_ref):
+        for place in range(2):
+            rows = slice(place * chunk, (place + 1) * chunk)
+            for target, index in ((send_ref, order_ref[place]), (keep_ref, order_ref[place + 2])):
+                source = pl.ds(pl.multiple_of(index * chunk, 8), chunk)
+                target[rows, :wide] = wide_ref[source, :].astype(target.dtype)
+                target[rows, wide:] = narrow_ref[source, :].astype(target.dtype)
+
+    def whole(rows, columns):
+        return pl.BlockSpec((rows, columns), lambda _: (0, 0))
+
+    return pl.pallas_call(
+        kernel,
+        grid=(1,),
+        out_shape=(
+            jax.ShapeDtypeStruct((2 * chunk, width), BF16),
+            jax.ShapeDtypeStruct((2 * chunk, width), F32),
+        ),
+        in_specs=[
+            pl.BlockSpec(memory_space=pltpu.SMEM),
+            whole(count, wide),
+            whole(count, width - wide),
+        ],
+        out_specs=(whole(2 * chunk, width), whole(2 * chunk, width)),
+        compiler_params=pltpu.CompilerParams(vmem_limit_bytes=16 << 20),
+        name="pick",
+    )(order, wide_part, narrow_part)
+
+
+def swap_row(value, stage):
+    size = lax.axis_size("row")
+    pairs = []
+    for row in range(size):
+        x, core = row // 2, row % 2
+        to_x = x ^ 1 if core == stage else size // 2 - 1 - x
+        pairs.append((row, 2 * to_x + core))
+    return lax.ppermute(value, "row", pairs)
+
+
+def sum_row(wide_part, narrow_part):
+    row = lax.axis_index("row")
+    x, core = row // 2, row % 2
+    mirrored = lax.axis_size("row") // 2 - 1 - x
+    first = jnp.where(core == 0, x ^ 1, mirrored)
+    second = jnp.where(core == 0, mirrored, x ^ 1)
+    last = lax.axis_size("row") // 2 - 1 - first
+    far = jnp.where(core == 0, last, first ^ 1)
+    send, keep = pick(jnp.stack([first, far, x, second]), wide_part, narrow_part)
+    chunk = keep.shape[0] // 2
+    keep = keep + swap_row(send, 0).astype(F32)
+    return keep[:chunk] + swap_row(keep[chunk:].astype(BF16), 1).astype(F32)
+
+
 def scatter_col(parts, rows):
     summed = lax.psum_scatter(
         parts, "col", scatter_dimension=0, tiled=True, axis_index_groups=every_other("col")
@@ -114,24 +172,13 @@
     weights_pair = move(weights, True, 0)
 
     wide = 2 * own
-    tall = 3 * own
     both_part = dot(rows_own[:, :features], weights[:wide], NT) + dot(
         rows_pair[:, :features], weights_pair[:wide], NT
     )
     back_part = dot(rows_own[:, features:], weights[wide:], NT) + dot(
         rows_pair[:, features:], weights_pair[wide:], NT
     )
-    parts = jnp.concatenate([both_part.astype(BF16), back_part.astype(BF16)], axis=1)
-    members = lax.axis_size("row") // 2
-    arrived = lax.all_to_all(
-        parts.reshape(members, count // members, tall),
-        "row",
-        0,
-        0,
-        axis_index_groups=every_other("row"),
-        tiled=True,
-    )
-    summed = jnp.sum(arrived.astype(F32), axis=0)
+    summed = sum_row(both_part, back_part)
     gate_val, up_val, back_hidden = (summed[:, k * own : (k + 1) * own] for k in range(3))
     gate_sig = jax.nn.sigmoid(gate_val)
     activation = gate_val * gate_sig

time: 218 us -> 225 us (1.032)
  waiting for transfers between devices: 20.4 us -> 13.7 us
  matrix products: 6.72 us -> 11.4 us
  blocking collectives: 145 us -> 149 us
  local copies, waits for them, and re-layouts: 4.76 us -> 7.19 us
    all_to_all x1 -> x0, waiting for transfers between devices: 11.4 us -> none  [layer(): lax.all_to_all(parts.reshape(members, count // members, tall), 'row', 0,...]
    ppermute x0 -> x2, starting transfers between devices: none -> 8.5 us  [swap_row(): return lax.ppermute(value, 'row', pairs)]
    ppermute x0 -> x2, waiting for transfers between devices: none -> 8.45 us  [swap_row(): return lax.ppermute(value, 'row', pairs)]
    dot_general x12, matrix products: 6.72 us -> 11.4 us  [dot(): return lax.dot_general(left, right, dims, preferred_element_type=F32)]
    all_to_all x1 -> x0, starting transfers between devices: 4.58 us -> none  [layer(): lax.all_to_all(parts.reshape(members, count // members, tall), 'row', 0,...]
    unnamed x1, blocking collectives: 51.3 us -> 55.6 us
    ppermute x8, waiting for transfers between devices: 8.55 us -> 4.9 us  [move(): return lax.ppermute(value, ('row', 'col'), pairs)]
  transfers between devices with their start and end apart: 10 -> 11, of which waited for: 5 -> 6; matrix products, arithmetic and copies ran while one was open for 26% -> 29% of each run, Pallas kernels for 0% -> 0%
where the time goes in v6:
time: 225 us
  blocking collectives  149 us (66%)
  starting transfers between devices  33 us (15%)
  waiting for transfers between devices  13.7 us (6%)
  matrix products  11.4 us (5%)
  local copies, waits for them, and re-layouts  7.19 us (3%)
  other arithmetic  6.73 us (3%)
  between operations  2.39 us (1%)
    all_gather x1, blocking collectives, gather_col(): lax.all_gather(block, 'col', axis=0, tiled=True, axis_index_groups=every_...  79.2 us
    unnamed x1, blocking collectives  55.6 us
    ppermute x8, starting transfers between devices, move(): return lax.ppermute(value, ('row', 'col'), pairs)  22.1 us
    all_gather x1, blocking collectives, layer(): lax.all_gather(jnp.concatenate([back_gate, back_up, hidden], axis=1), 'ro...  14.4 us
    dot_general x12, matrix products, dot(): return lax.dot_general(left, right, dims, preferred_element_type=F32)  11.4 us
    ppermute x2, starting transfers between devices, swap_row(): return lax.ppermute(value, 'row', pairs)  8.5 us
    ppermute x2, waiting for transfers between devices, swap_row(): return lax.ppermute(value, 'row', pairs)  8.45 us
    ppermute x8, waiting for transfers between devices, move(): return lax.ppermute(value, ('row', 'col'), pairs)  4.9 us
  transfers between devices with their start and end apart: 11, of which 6 were waited for; matrix products, arithmetic and copies ran while one was open for 29% of the time, Pallas kernels for 0%

profile of v6, /device:TPU:40, one launch (start us, length us, event | category | flops | bytes accessed | tf_op | source)
XLA Modules:
  0.0 224.5 jit_solution(16609917748810503348)
XLA Ops:
  0.7 0.8 maximum_bitcast_fusion
  1.4 79.2 %all-gather = bf16[16,20,1024]{2,1,0:T(8,128)(2,1)S(1)} all-gather(bf16[1,20,1024]{2,1,0:T(8,128)(2,1)S(1)} %maximum_bitcast_fusion), channel_id=1, replica_groups={{0,2,4,6,8,10,12,14,16,18,20,22,24,26,28,30},{1,3,5,7,9,11,13,15,17,19,..., dimensions={0}, use_global_device_ids=true | all-gather | bytes 696320 | tf_op jit(solution)/shard_map/all_gather | solution.py:46
  80.6 0.1 reshape.12
  80.7 0.9 constant_dynamic-slice_fusion.1
  81.6 0.3 copy-done.3
  81.9 0.2 copy-done.4
  82.1 0.1 pad_maximum_fusion
  82.2 2.0 collective-permute-start.3
  84.2 2.4 %collective-permute-start.1 = (bf16[160,1024]{1,0:T(8,128)(2,1)}, bf16[160,1024]{1,0:T(8,128)(2,1)}, u32[]{:S(2)}, u32[]{:S(2)}) collective-permute-start(bf16[160,1024]{1,0:T(8,128)(2,1)} %get-tuple-element.25), channel_id=1, source_target_pairs={{0,32},{1,33},{2,34},{3,35},{4,36},{5,37},{6,38},{7,39},{8,40},{9,... | collective-permute-start | bytes 983048 | tf_op jit(solution)/shard_map/ppermute | solution.py:42
  86.6 3.6 %collective-permute-start.2 = (bf16[160,1024]{1,0:T(8,128)(2,1)}, bf16[160,1024]{1,0:T(8,128)(2,1)}, u32[]{:S(2)}, u32[]{:S(2)}) collective-permute-start(bf16[160,1024]{1,0:T(8,128)(2,1)} %get-tuple-element.25), channel_id=1, source_target_pairs={{0,63},{1,32},{2,33},{3,34},{4,35},{5,36},{6,37},{7,38},{8,39},{9,... | collective-permute-start | bytes 983048 | tf_op jit(solution)/shard_map/ppermute | solution.py:42
  90.2 4.1 %collective-permute-start = (bf16[160,1024]{1,0:T(8,128)(2,1)}, bf16[160,1024]{1,0:T(8,128)(2,1)}, u32[]{:S(2)}, u32[]{:S(2)}) collective-permute-start(bf16[160,1024]{1,0:T(8,128)(2,1)} %get-tuple-element.22), channel_id=1, source_target_pairs={{0,1},{1,2},{2,3},{3,4},{4,5},{5,6},{6,7},{7,8},{8,9},{9,10},{10,1... | collective-permute-start | bytes 983048 | tf_op jit(solution)/shard_map/ppermute | solution.py:42
  94.4 1.0 constant_dynamic-update-slice_fusion.1
  95.4 0.1 pad_add_fusion.order_ref
  95.5 0.0 collective-permute-done.1
  95.5 1.0 constant_dynamic-update-slice_fusion.3
  96.5 0.1 collective-permute-done.2
  96.6 1.0 constant_dynamic-update-slice_fusion.2
  97.6 3.2 %collective-permute-done = bf16[160,1024]{1,0:T(8,128)(2,1)} collective-permute-done((bf16[160,1024]{1,0:T(8,128)(2,1)}, bf16[160,1024]{1,0:T(8,128)(2,1)}, u32[]{:S(2)}, u32[]{:S(2)}) %collective-permute-start) | collective-permute-done | bytes 327712 | tf_op jit(solution)/shard_map/ppermute | solution.py:42
  100.8 1.0 constant_dynamic-update-slice_fusion
  101.8 0.0 copy-start.2
  101.8 0.0 collective-permute-done.3
  101.8 1.9 fusion.2
  103.7 0.6 convolution_add_fusion.wide_ref
  104.3 0.0 copy-done.5
  104.3 1.4 fusion.11
  105.7 0.4 convolution_add_fusion.1.narrow_ref
  106.0 0.7 pick.1
  106.7 3.6 %collective-permute-start.4 = (bf16[160,1344]{1,0:T(8,128)(2,1)S(1)}, bf16[160,1344]{1,0:T(8,128)(2,1)S(1)}, u32[]{:S(2)}, u32[]{:S(2)}) collective-permute-start(bf16[160,1344]{1,0:T(8,128)(2,1)S(1)} %get-tuple-element.28), channel_id=1, source_target_pairs={{0,64},{32,224},{64,0},{96,160},{128,192},{160,96},{192,128},{224,... | collective-permute-start | bytes 1290248 | tf_op jit(solution)/shard_map/ppermute | solution.py:133
  110.3 6.7 %collective-permute-done.4 = bf16[160,1344]{1,0:T(8,128)(2,1)S(1)} collective-permute-done((bf16[160,1344]{1,0:T(8,128)(2,1)S(1)}, bf16[160,1344]{1,0:T(8,128)(2,1)S(1)}, u32[]{:S(2)}, u32[]{:S(2)}) %collective-permute-start.4) | collective-permute-done | bytes 430112 | tf_op jit(solution)/shard_map/ppermute | solution.py:133
  117.0 0.1 convert_add_fusion
  117.1 4.9 %collective-permute-start.5 = (bf16[80,1344]{1,0:T(8,128)(2,1)S(1)}, bf16[80,1344]{1,0:T(8,128)(2,1)}, u32[]{:S(2)}, u32[]{:S(2)}) collective-permute-start(bf16[80,1344]{1,0:T(8,128)(2,1)S(1)} %slice.213), channel_id=1, source_target_pairs={{0,192},{32,96},{64,128},{96,32},{128,64},{160,224},{192,0},{224,1... | collective-permute-start | bytes 645128 | tf_op jit(solution)/shard_map/ppermute | solution.py:133
  122.7 1.3 dynamic-slice.4
  124.7 1.7 collective-permute-done.5
  126.4 1.0 slice_add_fusion
  127.3 0.1 multiply_convert_fusion.3
  127.5 0.1 concatenate.32
  127.6 14.4 %all_gather.7 = bf16[320,1344]{1,0:T(8,128)(2,1)S(1)} all-gather(bf16[80,1344]{1,0:T(8,128)(2,1)S(1)} %concatenate.32), channel_id=1, replica_groups={{0,64,128,192},{32,96,160,224},{1,65,129,193},{33,97,161,225},{2,66,130..., dimensions={0}, use_global_device_ids=true | all-gather | bytes 1075200 | tf_op jit(solution)/shard_map/all_gather | solution.py:188
  142.0 0.3 fusion.15.out_ref
  142.3 0.5 fusion.4.grad_ref
  142.9 1.7 convolution_convert_fusion.2
  144.6 1.4 convolution_convert_fusion.3
  146.0 0.1 pad_maximum_fusion.5
  146.1 0.4 convolution_convert_fusion.1
  146.6 0.7 convolution_convert_fusion
  147.3 2.0 collective-permute-start.6
  149.2 2.0 collective-permute-start.7
  151.2 4.2 %collective-permute-start.8 = (bf16[160,1024]{1,0:T(8,128)(2,1)S(1)}, bf16[160,1024]{1,0:T(8,128)(2,1)S(1)}, u32[]{:S(2)}, u32[]{:S(2)}) collective-permute-start(bf16[160,1024]{1,0:T(8,128)(2,1)S(1)} %get-tuple-element.31), channel_id=1, source_target_pairs={{0,63},{1,32},{2,33},{3,34},{4,35},{5,36},{6,37},{7,38},{8,39},{9,... | collective-permute-start | bytes 983048 | tf_op jit(solution)/shard_map/ppermute | solution.py:42
  155.4 1.2 pad_maximum_fusion.1
  156.5 1.9 collective-permute-start.9
  158.5 0.7 fusion.8
  159.2 0.0 collective-permute-done.6.near_ref
  159.2 0.0 collective-permute-done.7.pair_ref
  159.2 1.6 collective-permute-done.8.far_ref
  160.8 0.3 spread.1
  161.1 55.6 %fusion = f32[24,1024]{1,0:T(8,128)S(1)} fusion(f32[368,1024]{1,0:T(8,128)S(1)} %spread.1), kind=kCustom, calls=%all-reduce-scatter | all-reduce-scatter fusion | flops 393217 | bytes 1607680
  216.8 2.3 %collective-permute-start.10 = (f32[15,1024]{1,0:T(8,128)S(1)}, f32[15,1024]{1,0:T(8,128)S(1)}, u32[]{:S(2)}, u32[]{:S(2)}) collective-permute-start(f32[15,1024]{1,0:T(8,128)S(1)} %slice.145), channel_id=1, source_target_pairs={{0,2},{2,4},{4,6},{6,8},{8,10},{10,12},{12,14},{14,16},{16,18},{18... | collective-permute-start | bytes 184328
  219.1 1.5 fusion.19
  220.6 0.4 collective-permute-done.10
  221.0 0.2 concatenate.36
  221.2 0.0 collective-permute-done.9
  221.2 0.0 copy-start.7
  221.2 0.0 copy-start.8
  221.2 2.7 %multiply_convert_fusion.1 = (bf16[448,512]{1,0:T(8,128)(2,1)}, bf16[448,512]{1,0:T(8,128)(2,1)}, bf16[448,512]{1,0:T(8,128)(2,1)}) fusion(f32[896,512]{1,0:T(8,128)S(1)} %fusion.8, bf16[1344,512]{1,0:T(8,128)(2,1)} %collective-permute-done.9, f32[]{:T(128)} %bitcast.8, f32[448,512]{1,0:T(8,128)S(1)} %fusion.19), kind=kLoop, calls=%fused_computation.10 | loop fusion | flops 2752512 | bytes 5505028 | tf_op jit(solution)/shard_map/convert_element_type | solution.py:227
  223.9 0.6 add_convert_fusion
  (17 shorter events, 0.1 us)
Async XLA Ops:
  80.6 1.0 copy-start.1
  80.6 1.3 copy-start.3
  80.6 1.5 copy-start.4
  82.2 19.6 %collective-permute-start.3 = (bf16[1344,512]{1,0:T(8,128)(2,1)S(1)}, bf16[1344,512]{1,0:T(8,128)(2,1)}, u32[]{:S(2)}, u32[]{:S(2)}) collective-permute-start(bf16[1344,512]{1,0:T(8,128)(2,1)S(1)} %pad_maximum_fusion), channel_id=1, source_target_pairs={{0,32},{1,33},{2,34},{3,35},{4,36},{5,37},{6,38},{7,39},{8,40},{9,... | collective-permute-start | bytes 4128776 | tf_op jit(solution)/shard_map/ppermute | solution.py:42
  84.2 11.3 %collective-permute-start.1 = (bf16[160,1024]{1,0:T(8,128)(2,1)}, bf16[160,1024]{1,0:T(8,128)(2,1)}, u32[]{:S(2)}, u32[]{:S(2)}) collective-permute-start(bf16[160,1024]{1,0:T(8,128)(2,1)} %get-tuple-element.25), channel_id=1, source_target_pairs={{0,32},{1,33},{2,34},{3,35},{4,36},{5,37},{6,38},{7,39},{8,40},{9,... | collective-permute-start | bytes 983048 | tf_op jit(solution)/shard_map/ppermute | solution.py:42
  86.6 10.0 %collective-permute-start.2 = (bf16[160,1024]{1,0:T(8,128)(2,1)}, bf16[160,1024]{1,0:T(8,128)(2,1)}, u32[]{:S(2)}, u32[]{:S(2)}) collective-permute-start(bf16[160,1024]{1,0:T(8,128)(2,1)} %get-tuple-element.25), channel_id=1, source_target_pairs={{0,63},{1,32},{2,33},{3,34},{4,35},{5,36},{6,37},{7,38},{8,39},{9,... | collective-permute-start | bytes 983048 | tf_op jit(solution)/shard_map/ppermute | solution.py:42
  90.2 10.5 %collective-permute-start = (bf16[160,1024]{1,0:T(8,128)(2,1)}, bf16[160,1024]{1,0:T(8,128)(2,1)}, u32[]{:S(2)}, u32[]{:S(2)}) collective-permute-start(bf16[160,1024]{1,0:T(8,128)(2,1)} %get-tuple-element.22), channel_id=1, source_target_pairs={{0,1},{1,2},{2,3},{3,4},{4,5},{5,6},{6,7},{7,8},{8,9},{9,10},{10,1... | collective-permute-start | bytes 983048 | tf_op jit(solution)/shard_map/ppermute | solution.py:42
  97.6 6.7 %copy-start.5 = (bf16[320,1024]{1,0:T(8,128)(2,1)}, bf16[320,1024]{1,0:T(8,128)(2,1)S(1)}, u32[]{:S(2)}) copy-start(bf16[320,1024]{1,0:T(8,128)(2,1)S(1)} %constant_dynamic-update-slice_fusion.2) | copy-start | bytes 1966084
  101.8 56.7 %copy-start.2 = (bf16[320,1024]{1,0:T(8,128)(2,1)}, bf16[320,1024]{1,0:T(8,128)(2,1)S(1)}, u32[]{:S(2)}) copy-start(bf16[320,1024]{1,0:T(8,128)(2,1)S(1)} %constant_dynamic-update-slice_fusion) | copy-start | bytes 1966084
  106.7 10.3 %collective-permute-start.4 = (bf16[160,1344]{1,0:T(8,128)(2,1)S(1)}, bf16[160,1344]{1,0:T(8,128)(2,1)S(1)}, u32[]{:S(2)}, u32[]{:S(2)}) collective-permute-start(bf16[160,1344]{1,0:T(8,128)(2,1)S(1)} %get-tuple-element.28), channel_id=1, source_target_pairs={{0,64},{32,224},{64,0},{96,160},{128,192},{160,96},{192,128},{224,... | collective-permute-start | bytes 1290248 | tf_op jit(solution)/shard_map/ppermute | solution.py:133
  117.1 9.2 %collective-permute-start.5 = (bf16[80,1344]{1,0:T(8,128)(2,1)S(1)}, bf16[80,1344]{1,0:T(8,128)(2,1)}, u32[]{:S(2)}, u32[]{:S(2)}) collective-permute-start(bf16[80,1344]{1,0:T(8,128)(2,1)S(1)} %slice.213), channel_id=1, source_target_pairs={{0,192},{32,96},{64,128},{96,32},{128,64},{160,224},{192,0},{224,1... | collective-permute-start | bytes 645128 | tf_op jit(solution)/shard_map/ppermute | solution.py:133
  142.0 16.5 %copy-start = (bf16[320,1344]{1,0:T(8,128)(2,1)}, bf16[320,1344]{1,0:T(8,128)(2,1)S(1)}, u32[]{:S(2)}) copy-start(bf16[320,1344]{1,0:T(8,128)(2,1)S(1)} %all_gather.7) | copy-start | bytes 2580484
  144.6 1.6 copy-start.6
  147.3 11.9 %collective-permute-start.6 = (bf16[160,1024]{1,0:T(8,128)(2,1)S(1)}, bf16[160,1024]{1,0:T(8,128)(2,1)S(1)}, u32[]{:S(2)}, u32[]{:S(2)}) collective-permute-start(bf16[160,1024]{1,0:T(8,128)(2,1)S(1)} %get-tuple-element.29), channel_id=1, source_target_pairs={{0,31},{1,0},{2,1},{3,2},{4,3},{5,4},{6,5},{7,6},{8,7},{9,8},{10,9... | collective-permute-start | bytes 983048 | tf_op jit(solution)/shard_map/ppermute | solution.py:42
  149.2 10.0 %collective-permute-start.7 = (bf16[160,1024]{1,0:T(8,128)(2,1)S(1)}, bf16[160,1024]{1,0:T(8,128)(2,1)S(1)}, u32[]{:S(2)}, u32[]{:S(2)}) collective-permute-start(bf16[160,1024]{1,0:T(8,128)(2,1)S(1)} %get-tuple-element.30), channel_id=1, source_target_pairs={{0,32},{1,33},{2,34},{3,35},{4,36},{5,37},{6,38},{7,39},{8,40},{9,... | collective-permute-start | bytes 983048 | tf_op jit(solution)/shard_map/ppermute | solution.py:42
  151.2 9.6 %collective-permute-start.8 = (bf16[160,1024]{1,0:T(8,128)(2,1)S(1)}, bf16[160,1024]{1,0:T(8,128)(2,1)S(1)}, u32[]{:S(2)}, u32[]{:S(2)}) collective-permute-start(bf16[160,1024]{1,0:T(8,128)(2,1)S(1)} %get-tuple-element.31), channel_id=1, source_target_pairs={{0,63},{1,32},{2,33},{3,34},{4,35},{5,36},{6,37},{7,38},{8,39},{9,... | collective-permute-start | bytes 983048 | tf_op jit(solution)/shard_map/ppermute | solution.py:42
  156.5 64.7 %collective-permute-start.9 = (bf16[1344,512]{1,0:T(8,128)(2,1)}, bf16[1344,512]{1,0:T(8,128)(2,1)}, u32[]{:S(2)}, u32[]{:S(2)}) collective-permute-start(bf16[1344,512]{1,0:T(8,128)(2,1)} %pad_maximum_fusion.1), channel_id=1, source_target_pairs={{0,32},{1,33},{2,34},{3,35},{4,36},{5,37},{6,38},{7,39},{8,40},{9,... | collective-permute-start | bytes 4128776 | tf_op jit(solution)/shard_map/ppermute | solution.py:42
  216.8 4.2 %collective-permute-start.10 = (f32[15,1024]{1,0:T(8,128)S(1)}, f32[15,1024]{1,0:T(8,128)S(1)}, u32[]{:S(2)}, u32[]{:S(2)}) collective-permute-start(f32[15,1024]{1,0:T(8,128)S(1)} %slice.145), channel_id=1, source_target_pairs={{0,2},{2,4},{4,6},{6,8},{8,10},{10,12},{12,14},{14,16},{16,18},{18... | collective-permute-start | bytes 184328
  221.2 2.7 %copy-start.7 = (bf16[20,512]{1,0:T(8,128)(2,1)S(1)}, bf16[20,512]{1,0:T(8,128)(2,1)}, u32[]{:S(2)}) copy-start(bf16[20,512]{1,0:T(8,128)(2,1)} %param.10) | copy-start | bytes 61444
  221.2 2.7 %copy-start.8 = (bf16[20,512]{1,0:T(8,128)(2,1)S(1)}, bf16[20,512]{1,0:T(8,128)(2,1)}, u32[]{:S(2)}) copy-start(bf16[20,512]{1,0:T(8,128)(2,1)} %param.6) | copy-start | bytes 61444

commit v7 on v5

--- a/solution.py
+++ b/solution.py
@@ -44,6 +44,35 @@
 
 def gather_col(block):
     return lax.all_gather(block, "col", axis=0, tiled=True, axis_index_groups=every_other("col"))
+
+
+def row_parts(rows_own, rows_pair, weights, weights_pair):
+    count, width = rows_own.shape
+    features = width // 2
+    tall = weights.shape[0]
+    wide = tall // 3 * 2
+    step = 256
+    edges = [*range(0, wide, step), *range(wide, tall, step), tall]
+
+    def kernel(own_ref, pair_ref, weights_ref, pair_weights_ref, parts_ref):
+        for low, high in zip(edges, edges[1:]):
+            columns = slice(0, features) if low < wide else slice(features, width)
+            total = dot(own_ref[:, columns], weights_ref[low:high, :], NT)
+            total += dot(pair_ref[:, columns], pair_weights_ref[low:high, :], NT)
+            parts_ref[:, low:high] = total.astype(BF16)
+
+    def whole(shape):
+        return pl.BlockSpec(shape, lambda _: (0, 0))
+
+    return pl.pallas_call(
+        kernel,
+        grid=(1,),
+        out_shape=jax.ShapeDtypeStruct((count, tall), BF16),
+        in_specs=[whole(v.shape) for v in (rows_own, rows_pair, weights, weights_pair)],
+        out_specs=whole((count, tall)),
+        compiler_params=pltpu.CompilerParams(vmem_limit_bytes=24 << 20),
+        name="row_parts",
+    )(rows_own, rows_pair, weights, weights_pair)
 
 
 def spread(core, out_own, grad_own, near, pair, far, rows, padded):
@@ -115,13 +144,7 @@
 
     wide = 2 * own
     tall = 3 * own
-    both_part = dot(rows_own[:, :features], weights[:wide], NT) + dot(
-        rows_pair[:, :features], weights_pair[:wide], NT
-    )
-    back_part = dot(rows_own[:, features:], weights[wide:], NT) + dot(
-        rows_pair[:, features:], weights_pair[wide:], NT
-    )
-    parts = jnp.concatenate([both_part.astype(BF16), back_part.astype(BF16)], axis=1)
+    parts = row_parts(rows_own, rows_pair, weights, weights_pair)
     members = lax.axis_size("row") // 2
     arrived = lax.all_to_all(
         parts.reshape(members, count // members, tall),

time: 218 us -> 220 us (level); the launches traced: 217 us -> 216 us
  Pallas kernels: 0.29 us -> 2.49 us
    unnamed x29 -> x25, local copies, waits for them, and re-layouts: 4.5 us -> 3.58 us
    dot_general x12 -> x8, matrix products: 6.72 us -> 6.11 us  [dot(): return lax.dot_general(left, right, dims, preferred_element_type=F32)]
  transfers between devices with their start and end apart: 10 -> 10, of which waited for: 5 -> 4; matrix products, arithmetic and copies ran while one was open for 26% -> 27% of each run, Pallas kernels for 0% -> 0%
where the time goes in v7:
time: 220 us; the launch traced here: 216 us
  blocking collectives  143 us (65%)
  starting transfers between devices  29.9 us (14%)
  waiting for transfers between devices  19.5 us (9%)
  other arithmetic  7.5 us (3%)
  matrix products  6.11 us (3%)
  local copies, waits for them, and re-layouts  4.73 us (2%)
  Pallas kernels  2.49 us (1%)
  between operations  2.3 us (1%)
    all_gather x1, blocking collectives, gather_col(): lax.all_gather(block, 'col', axis=0, tiled=True, axis_index_groups=every_...  79.2 us
    unnamed x1, blocking collectives  50.3 us
    ppermute x8, starting transfers between devices, move(): return lax.ppermute(value, ('row', 'col'), pairs)  23.2 us
    all_gather x1, blocking collectives, layer(): lax.all_gather(jnp.concatenate([back_gate, back_up, hidden], axis=1), 'ro...  13.7 us
    all_to_all x1, waiting for transfers between devices, layer(): lax.all_to_all(parts.reshape(members, count // members, tall), 'row', 0,...  9.77 us
    ppermute x8, waiting for transfers between devices, move(): return lax.ppermute(value, ('row', 'col'), pairs)  9.69 us
    dot_general x8, matrix products, dot(): return lax.dot_general(left, right, dims, preferred_element_type=F32)  6.11 us
    all_to_all x1, starting transfers between devices, layer(): lax.all_to_all(parts.reshape(members, count // members, tall), 'row', 0,...  4.58 us
  transfers between devices with their start and end apart: 10, of which 4 were waited for; matrix products, arithmetic and copies ran while one was open for 27% of the time, Pallas kernels for 0%

profile of v7, /device:TPU:40, one launch (start us, length us, event | category | flops | bytes accessed | tf_op | source)
XLA Modules:
  0.0 215.7 jit_solution(14141535151759336122)
XLA Ops:
  0.7 0.8 maximum_bitcast_fusion
  1.4 79.2 %all-gather = bf16[16,20,1024]{2,1,0:T(8,128)(2,1)S(1)} all-gather(bf16[1,20,1024]{2,1,0:T(8,128)(2,1)S(1)} %maximum_bitcast_fusion), channel_id=1, replica_groups={{0,2,4,6,8,10,12,14,16,18,20,22,24,26,28,30},{1,3,5,7,9,11,13,15,17,19,..., dimensions={0}, use_global_device_ids=true | all-gather | bytes 696320 | tf_op jit(solution)/shard_map/all_gather | solution.py:46
  80.6 0.0 copy-start.2
  80.6 0.0 copy-start.3
  80.6 0.0 copy-start.5
  80.6 0.1 reshape.16
  80.7 0.1 constant_dynamic-slice_fusion.1
  80.8 0.8 copy-done.2
  81.6 0.1 copy-done.3
  81.7 0.1 copy-done.5
  81.9 0.1 pad_maximum_fusion.weights_ref
  82.0 2.0 collective-permute-start.3
  83.9 2.4 %collective-permute-start.1 = (bf16[160,1024]{1,0:T(8,128)(2,1)S(1)}, bf16[160,1024]{1,0:T(8,128)(2,1)S(1)}, u32[]{:S(2)}, u32[]{:S(2)}) collective-permute-start(bf16[160,1024]{1,0:T(8,128)(2,1)S(1)} %get-tuple-element.21), channel_id=1, source_target_pairs={{0,32},{1,33},{2,34},{3,35},{4,36},{5,37},{6,38},{7,39},{8,40},{9,... | collective-permute-start | bytes 983048 | tf_op jit(solution)/shard_map/ppermute | solution.py:42
  86.4 5.8 %collective-permute-start = (bf16[160,1024]{1,0:T(8,128)(2,1)S(1)}, bf16[160,1024]{1,0:T(8,128)(2,1)S(1)}, u32[]{:S(2)}, u32[]{:S(2)}) collective-permute-start(bf16[160,1024]{1,0:T(8,128)(2,1)S(1)} %get-tuple-element.20), channel_id=1, source_target_pairs={{0,1},{1,2},{2,3},{3,4},{4,5},{5,6},{6,7},{7,8},{8,9},{9,10},{10,1... | collective-permute-start | bytes 983048 | tf_op jit(solution)/shard_map/ppermute | solution.py:42
  92.2 2.0 collective-permute-start.2
  94.1 0.0 collective-permute-done.1
  94.2 4.7 %collective-permute-done = bf16[160,1024]{1,0:T(8,128)(2,1)S(1)} collective-permute-done((bf16[160,1024]{1,0:T(8,128)(2,1)S(1)}, bf16[160,1024]{1,0:T(8,128)(2,1)S(1)}, u32[]{:S(2)}, u32[]{:S(2)}) %collective-permute-start) | collective-permute-done | bytes 327712 | tf_op jit(solution)/shard_map/ppermute | solution.py:42
  98.9 2.9 %collective-permute-done.2 = bf16[160,1024]{1,0:T(8,128)(2,1)S(1)} collective-permute-done((bf16[160,1024]{1,0:T(8,128)(2,1)S(1)}, bf16[160,1024]{1,0:T(8,128)(2,1)S(1)}, u32[]{:S(2)}, u32[]{:S(2)}) %collective-permute-start.2) | collective-permute-done | bytes 327712 | tf_op jit(solution)/shard_map/ppermute | solution.py:42
  101.8 0.0 collective-permute-done.3.pair_weights_ref
  101.8 2.2 %row_parts.1 = bf16[320,1344]{1,0:T(8,128)(2,1)} custom-call(bf16[320,1024]{1,0:T(8,128)(2,1)S(1)} %constant_dynamic-update-slice_fusion.own_ref, bf16[320,1024]{1,0:T(8,128)(2,1)S(1)} %constant_dynamic-update-slice_fusion.2.pair_ref, bf16[1344,512]{1,0:T(8,128)(2,1)S(1)} %pad_maximum_fusion.weights_ref, ...), custom_call_target="tpu_custom_call" | custom-call | tf_op jit(solution)/shard_map/row_parts/pallas_call | solution.py:67
  104.0 4.6 %all-to-all-start = ((bf16[4,80,1344]{2,1,0:T(8,128)(2,1)}), bf16[4,80,1344]{2,1,0:T(8,128)(2,1)}, u32[]{:S(2)}, u32[]{:S(2)}) async-start(bf16[4,80,1344]{2,1,0:T(8,128)(2,1)} %bitcast.4), calls=%async_computation | async-start | bytes 1802240 | tf_op jit(solution)/shard_map/all_to_all | solution.py:149
  109.3 1.3 dynamic-slice.4
  111.2 9.8 %all-to-all-done = bf16[4,80,1344]{2,1,0:T(8,128)(2,1)} async-done(((bf16[4,80,1344]{2,1,0:T(8,128)(2,1)}), bf16[4,80,1344]{2,1,0:T(8,128)(2,1)}, u32[]{:S(2)}, u32[]{:S(2)}) %all-to-all-start) | async-done | bytes 860192 | tf_op jit(solution)/shard_map/all_to_all | solution.py:149
  121.0 1.3 convert_reduce_fusion
  122.3 0.7 multiply_convert_fusion.3
  123.0 1.0 concatenate.31
  124.0 0.0 copy-start.4
  124.0 0.0 copy-start.6
  124.1 13.7 %all_gather.7 = bf16[320,1344]{1,0:T(8,128)(2,1)S(1)} all-gather(bf16[80,1344]{1,0:T(8,128)(2,1)S(1)} %concatenate.31), channel_id=1, replica_groups={{0,64,128,192},{32,96,160,224},{1,65,129,193},{33,97,161,225},{2,66,130..., dimensions={0}, use_global_device_ids=true | all-gather | bytes 1075200 | tf_op jit(solution)/shard_map/all_gather | solution.py:164
  137.8 0.0 copy-start.1
  137.8 0.3 fusion.19.out_ref
  138.1 0.0 copy-done.4
  138.1 0.0 copy-done.6
  138.1 0.5 fusion.2.grad_ref
  138.7 0.5 convolution_convert_fusion.2
  139.2 0.3 convolution_convert_fusion.3
  139.5 0.1 pad_maximum_fusion.2
  139.7 0.4 convolution_convert_fusion.1
  140.1 0.7 convolution_convert_fusion
  140.8 4.7 %collective-permute-start.4 = (bf16[160,1024]{1,0:T(8,128)(2,1)S(1)}, bf16[160,1024]{1,0:T(8,128)(2,1)S(1)}, u32[]{:S(2)}, u32[]{:S(2)}) collective-permute-start(bf16[160,1024]{1,0:T(8,128)(2,1)S(1)} %get-tuple-element.25), channel_id=1, source_target_pairs={{0,31},{1,0},{2,1},{3,2},{4,3},{5,4},{6,5},{7,6},{8,7},{9,8},{10,9... | collective-permute-start | bytes 983048 | tf_op jit(solution)/shard_map/ppermute | solution.py:42
  145.5 2.0 collective-permute-start.5
  147.5 2.1 collective-permute-start.6
  149.5 1.2 pad_maximum_fusion.1
  150.7 2.3 %collective-permute-start.7 = (bf16[1344,512]{1,0:T(8,128)(2,1)}, bf16[1344,512]{1,0:T(8,128)(2,1)}, u32[]{:S(2)}, u32[]{:S(2)}) collective-permute-start(bf16[1344,512]{1,0:T(8,128)(2,1)} %pad_maximum_fusion.1), channel_id=1, source_target_pairs={{0,32},{1,33},{2,34},{3,35},{4,36},{5,37},{6,38},{7,39},{8,40},{9,... | collective-permute-start | bytes 4128776 | tf_op jit(solution)/shard_map/ppermute | solution.py:42
  153.0 0.0 copy-done.1
  153.1 1.9 fusion.9
  155.0 0.0 collective-permute-done.4.near_ref
  155.0 0.0 collective-permute-done.5.pair_ref
  155.0 2.1 collective-permute-done.6.far_ref
  157.1 0.3 spread.1
  157.4 50.3 %fusion = f32[24,1024]{1,0:T(8,128)S(1)} fusion(f32[368,1024]{1,0:T(8,128)S(1)} %spread.1), kind=kCustom, calls=%all-reduce-scatter | all-reduce-scatter fusion | flops 393217 | bytes 1607680
  207.8 0.0 copy-start
  207.8 2.2 %collective-permute-start.8 = (f32[15,1024]{1,0:T(8,128)S(1)}, f32[15,1024]{1,0:T(8,128)}, u32[]{:S(2)}, u32[]{:S(2)}) collective-permute-start(f32[15,1024]{1,0:T(8,128)S(1)} %slice.127), channel_id=1, source_target_pairs={{0,2},{2,4},{4,6},{6,8},{8,10},{10,12},{12,14},{14,16},{16,18},{18... | collective-permute-start | bytes 184328
  210.0 1.4 fusion.15
  211.4 0.0 collective-permute-done.8
  211.4 1.0 concatenate.36
  212.4 0.0 collective-permute-done.7
  212.4 0.0 copy-done
  212.4 0.0 copy-start.7
  212.4 0.0 copy-start.8
  212.4 2.7 %multiply_convert_fusion.1 = (bf16[448,512]{1,0:T(8,128)(2,1)}, bf16[448,512]{1,0:T(8,128)(2,1)}, bf16[448,512]{1,0:T(8,128)(2,1)}) fusion(f32[896,512]{1,0:T(8,128)S(1)} %copy-done, bf16[1344,512]{1,0:T(8,128)(2,1)} %collective-permute-done.7, f32[]{:T(128)} %bitcast.5, f32[448,512]{1,0:T(8,128)S(1)} %fusion.15), kind=kLoop, calls=%fused_computation.13 | loop fusion | flops 2752512 | bytes 5505028 | tf_op jit(solution)/shard_map/convert_element_type | solution.py:203
  215.1 0.0 copy-done.7
  215.1 0.0 copy-done.8
  215.1 0.6 add_convert_fusion
  (8 shorter events, 0.2 us)
Async XLA Ops:
  80.6 1.0 copy-start.2
  80.6 1.2 copy-start.3
  80.6 1.3 copy-start.5
  82.0 19.9 %collective-permute-start.3 = (bf16[1344,512]{1,0:T(8,128)(2,1)S(1)}, bf16[1344,512]{1,0:T(8,128)(2,1)S(1)}, u32[]{:S(2)}, u32[]{:S(2)}) collective-permute-start(bf16[1344,512]{1,0:T(8,128)(2,1)S(1)} %pad_maximum_fusion.weights_ref), channel_id=1, source_target_pairs={{0,32},{1,33},{2,34},{3,35},{4,36},{5,37},{6,38},{7,39},{8,40},{9,... | collective-permute-start | bytes 4128776 | tf_op jit(solution)/shard_map/ppermute | solution.py:42
  83.9 10.2 %collective-permute-start.1 = (bf16[160,1024]{1,0:T(8,128)(2,1)S(1)}, bf16[160,1024]{1,0:T(8,128)(2,1)S(1)}, u32[]{:S(2)}, u32[]{:S(2)}) collective-permute-start(bf16[160,1024]{1,0:T(8,128)(2,1)S(1)} %get-tuple-element.21), channel_id=1, source_target_pairs={{0,32},{1,33},{2,34},{3,35},{4,36},{5,37},{6,38},{7,39},{8,40},{9,... | collective-permute-start | bytes 983048 | tf_op jit(solution)/shard_map/ppermute | solution.py:42
  86.4 12.5 %collective-permute-start = (bf16[160,1024]{1,0:T(8,128)(2,1)S(1)}, bf16[160,1024]{1,0:T(8,128)(2,1)S(1)}, u32[]{:S(2)}, u32[]{:S(2)}) collective-permute-start(bf16[160,1024]{1,0:T(8,128)(2,1)S(1)} %get-tuple-element.20), channel_id=1, source_target_pairs={{0,1},{1,2},{2,3},{3,4},{4,5},{5,6},{6,7},{7,8},{8,9},{9,10},{10,1... | collective-permute-start | bytes 983048 | tf_op jit(solution)/shard_map/ppermute | solution.py:42
  92.2 9.6 %collective-permute-start.2 = (bf16[160,1024]{1,0:T(8,128)(2,1)S(1)}, bf16[160,1024]{1,0:T(8,128)(2,1)S(1)}, u32[]{:S(2)}, u32[]{:S(2)}) collective-permute-start(bf16[160,1024]{1,0:T(8,128)(2,1)S(1)} %get-tuple-element.21), channel_id=1, source_target_pairs={{0,63},{1,32},{2,33},{3,34},{4,35},{5,36},{6,37},{7,38},{8,39},{9,... | collective-permute-start | bytes 983048 | tf_op jit(solution)/shard_map/ppermute | solution.py:42
  104.0 16.9 %all-to-all-start = ((bf16[4,80,1344]{2,1,0:T(8,128)(2,1)}), bf16[4,80,1344]{2,1,0:T(8,128)(2,1)}, u32[]{:S(2)}, u32[]{:S(2)}) async-start(bf16[4,80,1344]{2,1,0:T(8,128)(2,1)} %bitcast.4), calls=%async_computation | async-start | bytes 1802240 | tf_op jit(solution)/shard_map/all_to_all | solution.py:149
  124.0 14.1 %copy-start.4 = (bf16[512,448]{0,1:T(8,128)(2,1)S(1)}, bf16[512,448]{0,1:T(8,128)(2,1)}, u32[]{:S(2)}) copy-start(bf16[512,448]{0,1:T(8,128)(2,1)} %param.8) | copy-start | bytes 1376260
  124.0 14.1 %copy-start.6 = (bf16[512,448]{0,1:T(8,128)(2,1)S(1)}, bf16[512,448]{0,1:T(8,128)(2,1)}, u32[]{:S(2)}) copy-start(bf16[512,448]{0,1:T(8,128)(2,1)} %param.7) | copy-start | bytes 1376260
  137.8 15.3 %copy-start.1 = (bf16[320,1344]{1,0:T(8,128)(2,1)}, bf16[320,1344]{1,0:T(8,128)(2,1)S(1)}, u32[]{:S(2)}) copy-start(bf16[320,1344]{1,0:T(8,128)(2,1)S(1)} %all_gather.7) | copy-start | bytes 2580484
  140.8 14.2 %collective-permute-start.4 = (bf16[160,1024]{1,0:T(8,128)(2,1)S(1)}, bf16[160,1024]{1,0:T(8,128)(2,1)S(1)}, u32[]{:S(2)}, u32[]{:S(2)}) collective-permute-start(bf16[160,1024]{1,0:T(8,128)(2,1)S(1)} %get-tuple-element.25), channel_id=1, source_target_pairs={{0,31},{1,0},{2,1},{3,2},{4,3},{5,4},{6,5},{7,6},{8,7},{9,8},{10,9... | collective-permute-start | bytes 983048 | tf_op jit(solution)/shard_map/ppermute | solution.py:42
  145.5 9.5 %collective-permute-start.5 = (bf16[160,1024]{1,0:T(8,128)(2,1)S(1)}, bf16[160,1024]{1,0:T(8,128)(2,1)S(1)}, u32[]{:S(2)}, u32[]{:S(2)}) collective-permute-start(bf16[160,1024]{1,0:T(8,128)(2,1)S(1)} %get-tuple-element.26), channel_id=1, source_target_pairs={{0,32},{1,33},{2,34},{3,35},{4,36},{5,37},{6,38},{7,39},{8,40},{9,... | collective-permute-start | bytes 983048 | tf_op jit(solution)/shard_map/ppermute | solution.py:42
  147.5 9.6 %collective-permute-start.6 = (bf16[160,1024]{1,0:T(8,128)(2,1)S(1)}, bf16[160,1024]{1,0:T(8,128)(2,1)S(1)}, u32[]{:S(2)}, u32[]{:S(2)}) collective-permute-start(bf16[160,1024]{1,0:T(8,128)(2,1)S(1)} %get-tuple-element.27), channel_id=1, source_target_pairs={{0,63},{1,32},{2,33},{3,34},{4,35},{5,36},{6,37},{7,38},{8,39},{9,... | collective-permute-start | bytes 983048 | tf_op jit(solution)/shard_map/ppermute | solution.py:42
  150.7 61.7 %collective-permute-start.7 = (bf16[1344,512]{1,0:T(8,128)(2,1)}, bf16[1344,512]{1,0:T(8,128)(2,1)}, u32[]{:S(2)}, u32[]{:S(2)}) collective-permute-start(bf16[1344,512]{1,0:T(8,128)(2,1)} %pad_maximum_fusion.1), channel_id=1, source_target_pairs={{0,32},{1,33},{2,34},{3,35},{4,36},{5,37},{6,38},{7,39},{8,40},{9,... | collective-permute-start | bytes 4128776 | tf_op jit(solution)/shard_map/ppermute | solution.py:42
  207.8 4.6 %copy-start = (f32[896,512]{1,0:T(8,128)S(1)}, f32[896,512]{1,0:T(8,128)}, u32[]{:S(2)}) copy-start(f32[896,512]{1,0:T(8,128)} %fusion.9) | copy-start | bytes 5505028
  207.8 3.6 %collective-permute-start.8 = (f32[15,1024]{1,0:T(8,128)S(1)}, f32[15,1024]{1,0:T(8,128)}, u32[]{:S(2)}, u32[]{:S(2)}) collective-permute-start(f32[15,1024]{1,0:T(8,128)S(1)} %slice.127), channel_id=1, source_target_pairs={{0,2},{2,4},{4,6},{6,8},{8,10},{10,12},{12,14},{14,16},{16,18},{18... | collective-permute-start | bytes 184328
  212.4 2.7 %copy-start.7 = (bf16[20,512]{1,0:T(8,128)(2,1)S(1)}, bf16[20,512]{1,0:T(8,128)(2,1)}, u32[]{:S(2)}) copy-start(bf16[20,512]{1,0:T(8,128)(2,1)} %param.10) | copy-start | bytes 61444
  212.4 2.7 %copy-start.8 = (bf16[20,512]{1,0:T(8,128)(2,1)S(1)}, bf16[20,512]{1,0:T(8,128)(2,1)}, u32[]{:S(2)}) copy-start(bf16[20,512]{1,0:T(8,128)(2,1)} %param.6) | copy-start | bytes 61444
